TPU v7x, 512 devices: a whole 4x4x16 slice. The times are simulated.
512 devices in a mesh: dp: 8 (over y_hi, x), expert: 64 (over z, y_lo, core).
Axes of the slice: x: 4, y: 4 (y_hi: 2, y_lo: 2; y = y_hi * 2 + y_lo), z: 16, core: 2. Of those that a mesh axis runs over, the one named last changes fastest.
Arguments:
- tokens: bfloat16 [65536, 2048], P(('dp', 'expert')), may hold values from -6 to 6
- cotangent: bfloat16 [65536, 2048], P(('dp', 'expert')), may hold values from -6 to 6
- expert_ids: int32 [65536, 8], P(('dp', 'expert')), may hold values from 0 to 127, as said below
- gate_probs: float32 [65536, 8], P(('dp', 'expert')), may hold values from 0.1 to 1
- gate_weight: bfloat16 [64, 2048, 128], P('expert'), may hold values from -0.125 to 0.125
- up_weight: bfloat16 [64, 2048, 128], P('expert'), may hold values from -0.125 to 0.125
- down_weight: bfloat16 [64, 128, 2048], P('expert'), may hold values from -0.1875 to 0.1875
Outputs:
- grad_input: bfloat16 [65536, 2048], P(('dp', 'expert'))
- grad_gate: bfloat16 [64, 2048, 128], P('expert')
- grad_up: bfloat16 [64, 2048, 128], P('expert')
- grad_down: bfloat16 [64, 128, 2048], P('expert')
Inputs may be any that keep to these rules, and one draw needn't show every extreme that they name: `expert_ids`: each row names 8 different experts. Among the 128 rows of one device, each window expert 0 to 7 is named by 1 to 8 rows, and in every draw one window expert of every device is named by exactly 8 rows.
All inputs are finite; a program needn't handle non-finite values.
Results may differ from a plain program's by a relative error of at most 0.0064.
Values may be sent and summed in bfloat16 or wider, within the bound.
A program may use at most 64 MiB of HBM per device.

v0:
```python
import jax
import jax.numpy as jnp
from jax import lax
from jax.sharding import PartitionSpec as P

SLICES = 8
CAP = 8


def side_by_side(arrays, axis, split_dim, concat_dim, along):
    widths = [a.shape[along] for a in arrays]
    both = jnp.concatenate(arrays, axis=along)
    out = lax.all_to_all(both, axis, split_axis=split_dim, concat_axis=concat_dim, tiled=True)
    return tuple(jnp.split(out, [sum(widths[:k]) for k in range(1, len(widths))], axis=along))


def silu_parts(gate_pre):
    sigmoid_value = jax.nn.sigmoid(gate_pre)
    return (gate_pre * sigmoid_value, sigmoid_value * (1.0 + gate_pre * (1.0 - sigmoid_value)))


def expert_slice(rows_in, rows_cot, gate_rows, up_rows, down_rows):
    gate_pre = jnp.dot(rows_in, gate_rows, preferred_element_type=jnp.float32)
    upward = jnp.dot(rows_in, up_rows, preferred_element_type=jnp.float32)
    swish, slope = silu_parts(gate_pre)
    active = (swish * upward).astype(jnp.bfloat16)
    dhidden = lax.dot_general(
        rows_cot, down_rows, (((1,), (1,)), ((), ())), preferred_element_type=jnp.float32
    )
    dgate = (dhidden * upward * slope).astype(jnp.bfloat16)
    dupward = (dhidden * swish).astype(jnp.bfloat16)
    grad_down = lax.dot_general(
        active, rows_cot, (((0,), (0,)), ((), ())), preferred_element_type=jnp.float32
    )
    grad_gate = lax.dot_general(
        rows_in, dgate, (((0,), (0,)), ((), ())), preferred_element_type=jnp.float32
    )
    grad_up = lax.dot_general(
        rows_in, dupward, (((0,), (0,)), ((), ())), preferred_element_type=jnp.float32
    )
    partial_value = lax.dot_general(
        dgate, gate_rows, (((1,), (1,)), ((), ())), preferred_element_type=jnp.float32
    )
    partial_value = partial_value + lax.dot_general(
        dupward, up_rows, (((1,), (1,)), ((), ())), preferred_element_type=jnp.float32
    )
    return (partial_value, grad_gate, grad_up, grad_down)


def local(tokens, cotangent, expert_ids, gate_probs, gate_weight, up_weight, down_weight):
    devices = lax.axis_size("expert")
    window = devices // SLICES
    capacity = CAP
    width = tokens.shape[1]
    local_rows = tokens.shape[0]
    matched = expert_ids[:, :, None] == jnp.arange(window, dtype=jnp.int32)[None, None, :]
    hit_count = jnp.sum(matched.astype(jnp.int32), axis=1)
    chosen = jnp.sum(jnp.where(matched, gate_probs[:, :, None], 0.0), axis=1)
    slot_rank = jnp.cumsum(hit_count, axis=0) - hit_count
    placed = (hit_count[:, :, None] == 1) & (
        slot_rank[:, :, None] == jnp.arange(capacity, dtype=jnp.int32)[None, None, :]
    )
    picker = placed.astype(jnp.bfloat16)
    filled = jnp.any(placed, axis=0)
    owner_row = jnp.sum(
        jnp.where(placed, jnp.arange(local_rows, dtype=jnp.int32)[:, None, None], 0), axis=0
    )
    slot_prob = jnp.sum(jnp.where(placed, chosen[:, :, None], 0.0), axis=0)
    rows_in = jnp.einsum("tec,td->ecd", picker, tokens, preferred_element_type=jnp.float32).astype(
        jnp.bfloat16
    )
    picked_cot = jnp.einsum("tec,td->ecd", picker, cotangent, preferred_element_type=jnp.float32)
    rows_cot = (slot_prob[:, :, None] * picked_cot).astype(jnp.bfloat16)
    gate_rows = gate_weight[0]
    up_rows = up_weight[0]
    down_rows = down_weight[0]
    send_in = jnp.broadcast_to(rows_in[None], (SLICES, window, capacity, width)).reshape(
        devices, capacity, width
    )
    send_cot = jnp.broadcast_to(rows_cot[None], (SLICES, window, capacity, width)).reshape(
        devices, capacity, width
    )
    recv_in, recv_cot = side_by_side((send_in, send_cot), "expert", 0, 0, 1)
    partial_value, grad_g, grad_u, grad_d = expert_slice(
        recv_in.reshape(devices * capacity, width),
        recv_cot.reshape(devices * capacity, width),
        gate_rows,
        up_rows,
        down_rows,
    )
    returned = lax.all_to_all(
        partial_value.astype(jnp.bfloat16).reshape(devices, capacity, width),
        "expert",
        split_axis=0,
        concat_axis=0,
        tiled=True,
    )
    back = jnp.sum(returned.reshape(SLICES, window, capacity, width).astype(jnp.float32), axis=0)
    summed_g, summed_u, summed_d = lax.psum((grad_g, grad_u, grad_d), "dp")
    kept = jnp.where(filled[:, :, None], back, jnp.float32(0)).reshape(window * capacity, width)
    grad_rows = (
        jnp.zeros((local_rows, width), jnp.float32)
        .at[owner_row.reshape(window * capacity)]
        .add(kept)
    )
    grad_input = grad_rows.astype(jnp.bfloat16)
    return (
        grad_input,
        summed_g.astype(jnp.bfloat16)[None],
        summed_u.astype(jnp.bfloat16)[None],
        summed_d.astype(jnp.bfloat16)[None],
    )


def solution(mesh):
    placed = (
        P(("dp", "expert"), None),
        P(("dp", "expert"), None),
        P(("dp", "expert"), None),
        P(("dp", "expert"), None),
        P("expert", None, None),
        P("expert", None, None),
        P("expert", None, None),
    )
    return jax.shard_map(
        local,
        mesh=mesh,
        in_specs=placed,
        out_specs=(
            P(("dp", "expert"), None),
            P("expert", None, None),
            P("expert", None, None),
            P("expert", None, None),
        ),
        check_vma=False,
    )
```

profile of v0, /device:TPU:6, one launch (start us, length us, event | category | flops | bytes accessed | tf_op | source)
XLA Modules:
  0.0 332.9 jit_solution(5872676143290651411)
XLA Ops:
  0.6 0.0 copy-start
  0.6 0.8 convert_reduce_fusion.1
  1.4 0.1 copy.15
  1.5 0.7 select_reduce_fusion.1
  2.2 0.2 reduce_window_sum.11
  2.5 0.1 select_reduce_fusion
  2.6 1.3 convolution_convert_fusion
  3.8 1.3 fusion.1
  5.1 0.2 broadcast_in_dim.84
  5.4 0.3 broadcast_in_dim.88
  5.6 0.6 pad_maximum_fusion
  6.2 0.0 copy-start.3
  6.2 208.0 %all_to_all.10 = bf16[64,16,2048]{2,1,0:T(8,128)(2,1)S(1)} all-to-all(bf16[64,16,2048]{2,1,0:T(8,128)(2,1)S(1)} %pad_maximum_fusion), channel_id=1, replica_groups=mesh['dp'=8,'expert'=64] {'expert'}, dimensions={0} | all-to-all | bytes 8388608 | tf_op jit(solution)/shard_map/all_to_all | solution.py:13
  214.2 0.7 fusion.6
  215.0 0.7 fusion.7
  215.7 0.7 multiply_convert_fusion.1
  216.4 0.0 copy-done.1
  216.4 0.7 fusion.9
  217.1 2.1 fusion
  219.2 4.7 %all-to-all-start.1 = ((bf16[64,8,2048]{2,1,0:T(8,128)(2,1)}), bf16[64,8,2048]{2,1,0:T(8,128)(2,1)S(1)}, u32[]{:S(2)}, u32[]{:S(2)}) async-start(bf16[64,8,2048]{2,1,0:T(8,128)(2,1)} %fusion), calls=%async_computation.1 | async-start | bytes 4194304 | tf_op jit(solution)/shard_map/all_to_all | solution.py:91
  223.9 0.2 fusion.25
  224.1 0.1 broadcast_in_dim.82
  224.2 0.2 select_reduce_fusion.2
  224.4 0.1 reshape.81
  224.5 3.2 fusion.2
  227.7 3.3 %fusion.5 = f32[2048,128]{1,0:T(8,128)} fusion(bf16[512,128]{1,0:T(8,128)(2,1)S(1)} %get-tuple-element.8, bf16[64,16,2048]{2,1,0:T(8,128)(2,1)} %copy-done.1), kind=kOutput, calls=%fused_computation.13 | convolution fusion | flops 268435456 | bytes 3276800 | tf_op jit(solution)/shard_map/dot_general | solution.py:35
  231.1 1.7 fusion.4
  232.8 97.1 %all-reduce.2 = (bf16[2048,128]{1,0:T(8,128)(2,1)}, bf16[2048,128]{1,0:T(8,128)(2,1)}, bf16[128,2048]{1,0:T(8,128)(2,1)}) all-reduce(f32[2048,128]{1,0:T(8,128)} %fusion.5, f32[2048,128]{1,0:T(8,128)} %fusion.4, f32[128,2048]{1,0:T(8,128)} %fusion.2), channel_id=1, replica_groups=mesh['dp'=8,'expert'=64] {'dp'}, use_global_device_ids=true, to_apply=%region_8.9 | all-reduce | flops 786432 | bytes 4718592 | tf_op jit(solution)/shard_map/psum | solution.py:99
  329.9 0.0 all-to-all-done.1
  329.9 0.3 convert_reduce_fusion
  330.3 1.7 scatter_custom_fusion
  332.0 0.9 convert_element_type.48
  (11 shorter events, 0.1 us)
Async XLA Ops:
  0.6 213.6 %copy-start = (bf16[1,2048,128]{2,1,0:T(8,128)(2,1)S(1)}, bf16[1,2048,128]{2,1,0:T(8,128)(2,1)}, u32[]{:S(2)}) copy-start(bf16[1,2048,128]{2,1,0:T(8,128)(2,1)} %param.11) | copy-start | bytes 1572868
  6.2 208.7 %copy-start.3 = (bf16[1,2048,128]{2,1,0:T(8,128)(2,1)S(1)}, bf16[1,2048,128]{2,1,0:T(8,128)(2,1)}, u32[]{:S(2)}) copy-start(bf16[1,2048,128]{2,1,0:T(8,128)(2,1)} %param.12) | copy-start | bytes 1572868
  214.2 2.2 copy-start.1
  214.2 1.5 copy-start.4
  219.2 110.7 %all-to-all-start.1 = ((bf16[64,8,2048]{2,1,0:T(8,128)(2,1)}), bf16[64,8,2048]{2,1,0:T(8,128)(2,1)S(1)}, u32[]{:S(2)}, u32[]{:S(2)}) async-start(bf16[64,8,2048]{2,1,0:T(8,128)(2,1)} %fusion), calls=%async_computation.1 | async-start | bytes 4194304 | tf_op jit(solution)/shard_map/all_to_all | solution.py:91
  224.5 6.6 %copy-start.2 = (bf16[64,16,2048]{2,1,0:T(8,128)(2,1)S(1)}, bf16[64,16,2048]{2,1,0:T(8,128)(2,1)}, u32[]{:S(2)}) copy-start(bf16[64,16,2048]{2,1,0:T(8,128)(2,1)} %copy-done.1) | copy-start | bytes 12582916
where the time goes:
time: 335 us; the launch traced here: 333 us
  blocking collectives  305 us (91%)
  matrix products  15.7 us (5%)
  other arithmetic  5.72 us (2%)
  starting transfers between devices  4.69 us (1%)
    all_to_all x1, blocking collectives, side_by_side(): lax.all_to_all(both, axis, split_axis=split_dim, concat_axis=concat_dim,...  208 us
    psum x1, blocking collectives, local(): summed_g, summed_u, summed_d = lax.psum((grad_g, grad_u, grad_d), 'dp')  97.1 us
  transfers between devices with their start and end apart: 1, of which 0 were waited for; matrix products, arithmetic and copies ran while one was open for 3% of the time, Pallas kernels for 0%

commit v1 on v0

v1 whole, which is shorter than its diff:
```python
import jax
import jax.numpy as jnp
from jax import lax
from jax.sharding import PartitionSpec as P

SLICES = 8
CAP = 8
BF = jnp.bfloat16
F32 = jnp.float32


def local(tokens, cotangent, expert_ids, gate_probs, gate_weight, up_weight, down_weight):
    devices = lax.axis_size("expert")
    window = devices // SLICES
    cell = [[s * window + e for e in range(window)] for s in range(SLICES)]
    column = [[s * window + e for s in range(SLICES)] for e in range(window)]
    dp = lax.axis_size("dp")
    me = lax.axis_index("dp")
    width = tokens.shape[1]
    rows = tokens.shape[0]
    hid = down_weight.shape[1]
    piece = hid // dp
    gate_piece = lax.dynamic_slice(gate_weight[0], (0, me * piece), (width, piece)).T
    up_piece = lax.dynamic_slice(up_weight[0], (0, me * piece), (width, piece)).T
    down_piece = lax.dynamic_slice(down_weight[0], (me * piece, 0), (piece, width))
    weights = jnp.stack([gate_piece, up_piece, down_piece])
    weights = lax.all_gather(weights, "expert", axis=1, axis_index_groups=column)
    weights = weights.reshape(3 * hid, width)

    matched = expert_ids[:, :, None] == jnp.arange(window, dtype=jnp.int32)[None, None, :]
    hit = jnp.sum(matched.astype(jnp.int32), axis=1)
    chosen = jnp.sum(jnp.where(matched, gate_probs[:, :, None], 0.0), axis=1)
    rank = jnp.cumsum(hit, axis=0) - hit
    placed = (hit[:, :, None] == 1) & (
        rank[:, :, None] == jnp.arange(CAP, dtype=jnp.int32)[None, None, :]
    )
    picker = placed.astype(BF)
    slot_prob = jnp.sum(jnp.where(placed, chosen[:, :, None], 0.0), axis=0)
    rows_in = jnp.einsum("tec,td->ecd", picker, tokens, preferred_element_type=F32).astype(BF)
    picked = jnp.einsum("tec,td->ecd", picker, cotangent, preferred_element_type=F32)
    rows_cot = (slot_prob[:, :, None] * picked).astype(BF)
    message = jnp.concatenate([rows_in, rows_cot], axis=1)
    message = lax.all_to_all(
        message, "expert", split_axis=0, concat_axis=0, axis_index_groups=cell, tiled=True
    )
    both = lax.all_gather(message, "dp", axis=0)
    blocks = dp * window
    both = both.reshape(blocks * 2 * CAP, width)

    first = lax.dot_general(both, weights, (((1,), (1,)), ((), ())), preferred_element_type=F32)
    first = first.reshape(blocks, 2, CAP, 3, hid)
    pre = first[:, 0, :, 0]
    upward = first[:, 0, :, 1]
    dhidden = first[:, 1, :, 2]
    sigmoid = jax.nn.sigmoid(pre)
    swish = pre * sigmoid
    slope = sigmoid * (1.0 + pre * (1.0 - sigmoid))
    active = (swish * upward).astype(BF)
    dgate = (dhidden * upward * slope).astype(BF)
    dupward = (dhidden * swish).astype(BF)
    zero = jnp.zeros_like(active)
    left = jnp.concatenate(
        [
            jnp.concatenate([dgate, dupward, zero], axis=2),
            jnp.concatenate([zero, zero, active], axis=2),
        ],
        axis=1,
    ).reshape(blocks * 2 * CAP, 3 * hid)
    grads = lax.dot_general(left, both, (((0,), (0,)), ((), ())), preferred_element_type=F32)
    pair = jnp.concatenate([dgate, dupward], axis=2).reshape(blocks * CAP, 2 * hid)
    part = jnp.dot(pair, weights[: 2 * hid], preferred_element_type=F32).astype(BF)

    grads = grads.astype(BF).reshape(3, SLICES, piece, width).transpose(1, 0, 2, 3)
    grads = lax.psum_scatter(
        grads.reshape(SLICES * 3 * piece, width),
        "expert",
        scatter_dimension=0,
        axis_index_groups=column,
        tiled=True,
    ).reshape(3, piece, width)
    grads = lax.all_gather(grads, "dp", axis=1).reshape(3, hid, width)

    part = part.reshape(dp, window, CAP, width)
    part = lax.psum_scatter(part, "dp", scatter_dimension=0, tiled=False)
    back = lax.all_to_all(
        part, "expert", split_axis=0, concat_axis=0, axis_index_groups=cell, tiled=True
    )
    grad_input = lax.dot_general(
        picker.reshape(rows, window * CAP),
        back.reshape(window * CAP, width),
        (((1,), (0,)), ((), ())),
        preferred_element_type=F32,
    ).astype(BF)
    return (grad_input, grads[0].T[None], grads[1].T[None], grads[2][None])


def solution(mesh):
    tok = P(("dp", "expert"), None)
    wgt = P("expert", None, None)
    return jax.shard_map(
        local,
        mesh=mesh,
        in_specs=(tok, tok, tok, tok, wgt, wgt, wgt),
        out_specs=(tok, wgt, wgt, wgt),
        check_vma=False,
    )
```

time: 335 us -> 398 us (1.19)
  waiting for transfers between devices: 0.01 us -> 339 us
  blocking collectives: 305 us -> 22.5 us
  between operations: 0.77 us -> 13.9 us
  local copies, waits for them, and re-layouts: 0.84 us -> 9.55 us
  matrix products: 15.7 us -> 10.2 us
  starting transfers between devices: 4.69 us -> 0.21 us
  other arithmetic: 5.72 us -> 1.48 us
    all_gather x0 -> x3, waiting for transfers between devices: none -> 191 us  [the longest x1 83.7 us: local(): both = lax.all_gather(message, 'dp', axis=0)]
    all_to_all x1 -> x2, blocking collectives: 208 us -> 22.5 us  [the longest x1 13.1 us: local(): lax.all_to_all(message, 'expert', split_axis=0, concat_axis=0, axis_index...]
    reduce_scatter x0 -> x2, waiting for transfers between devices: none -> 148 us  [the longest x1 92.7 us: local(): part = lax.psum_scatter(part, 'dp', scatter_dimension=0, tiled=False)]
    psum x1 -> x0, blocking collectives: 97.1 us -> none  [local(): summed_g, summed_u, summed_d = lax.psum((grad_g, grad_u, grad_d), 'dp')]
    dot_general x10 -> x6, matrix products: 15.7 us -> 10.2 us  [the longest x1 4.74 us: local(): lax.dot_general(both, weights, (((1,), (1,)), ((), ())), preferred_elemen...]
    all_to_all x1 -> x0, starting transfers between devices: 4.69 us -> none  [local(): lax.all_to_all(partial_value.astype(jnp.bfloat16).reshape(devices, capaci...]
  transfers between devices with their start and end apart: 1 -> 5, of which waited for: 0 -> 5; matrix products, arithmetic and copies ran while one was open for 3% -> 1% of each run, Pallas kernels for 0% -> 0%
where the time goes in v1:
time: 398 us; the launch traced here: 397 us
  waiting for transfers between devices  339 us (85%)
  blocking collectives  22.5 us (6%)
  between operations  13.9 us (3%)
  matrix products  10.2 us (3%)
  local copies, waits for them, and re-layouts  9.55 us (2%)
    reduce_scatter x1, waiting for transfers between devices, local(): part = lax.psum_scatter(part, 'dp', scatter_dimension=0, tiled=False)  92.7 us
    all_gather x1, waiting for transfers between devices, local(): both = lax.all_gather(message, 'dp', axis=0)  83.7 us
    all_gather x1, waiting for transfers between devices, local(): grads = lax.all_gather(grads, 'dp', axis=1).reshape(3, hid, width)  57.9 us
    reduce_scatter x1, waiting for transfers between devices, local(): lax.psum_scatter(grads.reshape(SLICES * 3 * piece, width), 'expert', scat...  55.3 us
    all_gather x1, waiting for transfers between devices, local(): lax.all_gather(weights, 'expert', axis=1, axis_index_groups=column)  49.7 us
    all_to_all x1, blocking collectives, local(): lax.all_to_all(message, 'expert', split_axis=0, concat_axis=0, axis_index...  13.1 us
    all_to_all x1, blocking collectives, local(): lax.all_to_all(part, 'expert', split_axis=0, concat_axis=0, axis_index_gr...  9.43 us
  transfers between devices with their start and end apart: 5, of which 5 were waited for; matrix products, arithmetic and copies ran while one was open for 1% of the time, Pallas kernels for 0%

profile of v1, /device:TPU:6, one launch (start us, length us, event | category | flops | bytes accessed | tf_op | source)
XLA Modules:
  0.0 397.3 jit_solution(2477589647719683832)
XLA Ops:
  7.2 0.9 constant_dynamic-slice_fusion
  8.1 1.6 constant_dynamic-slice_fusion.1
  9.7 0.2 copy.33
  9.9 0.2 copy.32
  10.1 0.7 pad_maximum_fusion.1
  10.8 0.0 all-gather.8.cloned.1.call-start
  10.9 0.1 copy.29
  11.0 0.2 reduce_window_sum.11
  11.3 0.1 select_reduce_fusion
  11.4 0.2 convolution_convert_fusion.2
  11.6 0.2 fusion.3
  11.9 13.1 %all_to_all.10 = bf16[8,16,2048]{2,1,0:T(8,128)(2,1)} all-to-all(bf16[8,16,2048]{2,1,0:T(8,128)(2,1)S(1)} %pad_maximum_fusion), channel_id=1, replica_groups={{0,1,2,3,4,5,6,7},{8,9,10,11,12,13,14,15},{16,17,18,19,20,21,22,23},{24..., dimensions={0} | all-to-all | bytes 1048576 | tf_op jit(solution)/shard_map/all_to_all | solution.py:43
  25.1 49.7 %all-gather.10.cloned.1.call-done = bf16[3,128,2048]{2,1,0:T(8,128)(2,1)} async-done(((bf16[3,16,2048]{2,1,0:T(8,128)(2,1)}), bf16[3,128,2048]{2,1,0:T(8,128)(2,1)}) %all-gather.10.cloned.1.call-update) | async-done | bytes 1572880 | tf_op jit(solution)/shard_map/all_gather | solution.py:27
  74.8 83.7 %all-gather.8.cloned.1.call-done = bf16[64,16,2048]{2,1,0:T(8,128)(2,1)} async-done(((bf16[8,16,2048]{2,1,0:T(8,128)(2,1)}), bf16[64,16,2048]{2,1,0:T(8,128)(2,1)}) %all-gather.8.cloned.1.call-update) | async-done | bytes 4194320 | tf_op jit(solution)/shard_map/all_gather | solution.py:46
  158.5 4.7 %fusion = f32[64,2,8,3,128]{4,2,3,1,0:T(8,128)S(1)} fusion(bf16[64,16,2048]{2,1,0:T(8,128)(2,1)} %all-gather.8.cloned.1.call-done, bf16[3,128,2048]{2,1,0:T(8,128)(2,1)} %all-gather.10.cloned.1.call-done), kind=kOutput, calls=%fused_computation | convolution fusion | flops 1610612736 | bytes 7340032 | tf_op jit(solution)/shard_map/dot_general | solution.py:50
  163.3 0.2 fusion.13
  163.4 0.1 fusion.6
  163.5 1.8 convolution_convert_fusion.1
  165.4 1.2 copy.36
  166.7 0.0 reduce-scatter.3.cloned.1.call-start
  166.7 0.1 fusion.17
  166.9 1.0 slice-done
  167.9 2.1 convolution_convert_fusion
  170.0 0.0 all-gather.6.cloned.1.call-start
  170.0 55.3 %reduce-scatter.5.cloned.1.call-done = bf16[48,2048]{1,0:T(8,128)(2,1)} async-done(((bf16[384,2048]{1,0:T(8,128)(2,1)}), bf16[48,2048]{1,0:T(8,128)(2,1)}) %reduce-scatter.5.cloned.1.call-update) | async-done | bytes 196624 | tf_op jit(solution)/shard_map/reduce_scatter | solution.py:74
  225.3 92.7 %reduce-scatter.3.cloned.1.call-done = bf16[1,8,8,2048]{3,2,1,0:T(8,128)(2,1)} async-done(((bf16[8,8,8,2048]{3,2,1,0:T(8,128)(2,1)}), bf16[1,8,8,2048]{3,2,1,0:T(8,128)(2,1)}) %reduce-scatter.3.cloned.1.call-update) | async-done | bytes 262160 | tf_op jit(solution)/shard_map/reduce_scatter | solution.py:84
  318.0 9.4 %all_to_all.11 = bf16[8,8,2048]{2,1,0:T(8,128)(2,1)S(1)} all-to-all(bf16[8,8,2048]{2,1,0:T(8,128)(2,1)} %bitcast.144), channel_id=1, replica_groups={{0,1,2,3,4,5,6,7},{8,9,10,11,12,13,14,15},{16,17,18,19,20,21,22,23},{24..., dimensions={0} | all-to-all | bytes 524288 | tf_op jit(solution)/shard_map/all_to_all | solution.py:85
  327.4 1.1 fusion.2
  328.5 57.9 %all-gather.6.cloned.1.call-done = bf16[3,8,16,2048]{3,2,1,0:T(8,128)(2,1)} async-done(((bf16[3,1,16,2048]{3,2,1,0:T(8,128)(2,1)}), bf16[3,8,16,2048]{3,2,1,0:T(8,128)(2,1)}) %all-gather.6.cloned.1.call-update) | async-done | bytes 1572880 | tf_op jit(solution)/shard_map/all_gather | solution.py:81
  386.5 2.3 fusion.40
  388.7 1.0 copy.39
  389.7 1.0 copy.38
  (26 shorter events, 0.3 us)
Async XLA Ops:
  7.2 4.2 %copy-start = (bf16[128,2048]{1,0:T(8,128)(2,1)S(1)}, bf16[128,2048]{1,0:T(8,128)(2,1)}, u32[]{:S(2)}) copy-start(bf16[128,2048]{1,0:T(8,128)(2,1)} %param.7) | copy-start | bytes 1572868
  7.2 67.6 %all-gather.10.cloned.1.call-start = ((), (), s32[]{:S(2)}) async-start(), calls=%async_computation.8 | async-start | bytes 1769472 | tf_op jit(solution)/shard_map/all_gather | solution.py:27
  8.1 2.7 copy-start.2
  9.7 1.5 copy-start.3
  9.7 1.9 copy-start.1
  10.8 147.7 %all-gather.8.cloned.1.call-start = ((), (), s32[]{:S(2)}) async-start(), calls=%async_computation.7 | async-start | bytes 4718592 | tf_op jit(solution)/shard_map/all_gather | solution.py:46
  25.0 200.3 %reduce-scatter.5.cloned.1.call-start = ((), (), s32[]{:S(2)}) async-start(), calls=%async_computation.5 | async-start | bytes 1769472 | tf_op jit(solution)/shard_map/reduce_scatter | solution.py:74
  158.5 5.0 %copy-start.4 = (bf16[64,16,2048]{2,1,0:T(8,128)(2,1)S(1)}, bf16[64,16,2048]{2,1,0:T(8,128)(2,1)}, u32[]{:S(2)}) copy-start(bf16[64,16,2048]{2,1,0:T(8,128)(2,1)} %all-gather.8.cloned.1.call-done) | copy-start | bytes 12582916
  166.7 1.2 slice-start
  166.7 151.3 %reduce-scatter.3.cloned.1.call-start = ((), (), s32[]{:S(2)}) async-start(), calls=%async_computation.4 | async-start | bytes 2359296 | tf_op jit(solution)/shard_map/reduce_scatter | solution.py:84
  170.0 216.5 %all-gather.6.cloned.1.call-start = ((), (), s32[]{:S(2)}) async-start(), calls=%async_computation.6 | async-start | bytes 1769472 | tf_op jit(solution)/shard_map/all_gather | solution.py:81
Sparse Core Ops, SparseCore 0:
  10.9 63.8 all-gather.9
  78.0 80.4 all-gather.7
  166.8 58.4 reduce-scatter.4
  229.8 88.1 reduce-scatter.2
  321.0 65.3 all-gather.5

commit v2 on v1

v2 whole, which is shorter than its diff:
```python
import jax
import jax.numpy as jnp
from jax import lax
from jax.experimental import pallas as pl
from jax.experimental.pallas import tpu as pltpu
from jax.sharding import PartitionSpec as P

SLICES = 8
CAP = 8
XS = 4
BF = jnp.bfloat16
F32 = jnp.float32
MESH = pl.DeviceIdType.MESH
DMA = pltpu.SemaphoreType.DMA
FLIPS = [(fz, fy, fc) for fz in (0, 1) for fy in (0, 1) for fc in (0, 1)]


def kernel(
    ids_ref,
    probs_ref,
    tok_hbm,
    cot_hbm,
    gate_hbm,
    up_hbm,
    down_hbm,
    gi_ref,
    fg,
    tok,
    cot,
    gate,
    up,
    down,
    msg,
    x_all,
    w_all,
    lt,
    pair,
    grad,
    part,
    zs,
    zr,
    ps0,
    pr0,
    ps1,
    pr1,
    ys,
    yr,
    bs,
    br,
    load_sem,
    za_s,
    za_r,
    ca_s,
    ca_r,
    ya_s,
    ya_r,
    xa_s,
    xa_r,
    xb_s,
    xb_r,
    zg_s,
    zg_r,
    p0_s,
    p0_r,
    p1_s,
    p1_r,
    yb_s,
    yb_r,
    cb_s,
    cb_r,
    yg_s,
    yg_r,
    xg_s,
    xg_r,
    xh_s,
    xh_r,
):
    width = tok.shape[1]
    half = width // 2
    dp = lax.axis_index("dp")
    ex = lax.axis_index("expert")
    s = ex // 8
    e = ex % 8
    zb, yl, co = e // 4, (e // 2) % 2, e % 2
    x, yh = dp % XS, dp // XS
    oyh = 1 - yh

    def ring(k):
        return (s + k + 8) % 8

    def flip(f):
        fz, fy, fc = f
        return ((zb + fz) % 2) * 4 + ((yl + fy) % 2) * 2 + (co + fc) % 2

    def group(j):
        return ((zb + j // 2) % 2) * 2 + (yl + j % 2) % 2

    def dpx(rel, k):
        return (oyh if rel else yh) * XS + (x + k + XS) % XS

    z_to = [(dp, ring(1) * 8 + e), (dp, ring(-1) * 8 + e)]
    x_to = [(dpx(0, 1), ex), (dpx(0, -1), ex)]
    y_to = (dpx(1, 0), ex)
    c_to = [(dp, s * 8 + flip(f)) for f in FLIPS]
    sends = []

    def send(src, dst, ssem, rsem, to):
        c = pltpu.make_async_remote_copy(
            src_ref=src, dst_ref=dst, send_sem=ssem, recv_sem=rsem, device_id=to, device_id_type=MESH
        )
        c.start()
        sends.append(c)

    def arrive(dst, ssem, rsem, frm):
        pltpu.make_async_remote_copy(
            src_ref=dst, dst_ref=dst, send_sem=ssem, recv_sem=rsem, device_id=frm, device_id_type=MESH
        ).wait_recv()

    loads = [
        pltpu.make_async_copy(a, b, load_sem.at[i])
        for i, (a, b) in enumerate(
            [(gate_hbm.at[0], gate), (up_hbm.at[0], up), (down_hbm.at[0], down), (tok_hbm, tok), (cot_hbm, cot)]
        )
    ]
    for c in loads:
        c.start()

    barrier = pltpu.get_barrier_semaphore()
    partners = z_to + x_to + [y_to] + c_to[1:]
    for to in partners:
        pl.semaphore_signal(barrier, inc=1, device_id=to, device_id_type=MESH)

    row = lax.broadcasted_iota(jnp.int32, (16, 128), 0)
    lane = lax.broadcasted_iota(jnp.int32, (16, 128), 1)
    sel = jnp.where(lane == row + dp * 16, 1.0, 0.0).astype(BF)
    loads[0].wait()
    w_all[0, s] = lax.dot_general(
        sel, gate[...], (((1,), (1,)), ((), ())), preferred_element_type=F32
    ).astype(BF)
    loads[1].wait()
    w_all[1, s] = lax.dot_general(
        sel, up[...], (((1,), (1,)), ((), ())), preferred_element_type=F32
    ).astype(BF)
    loads[2].wait()
    w_all[2, s] = down[pl.ds(pl.multiple_of(dp * 16, 16), 16), :]
    pl.semaphore_wait(barrier, len(partners))

    def w_send(dr, k, t):
        c = ring(-k if dr == 0 else k)
        ref = w_all.at[t, c] if k < 3 else w_all.at[t, c, :, pl.ds(dr * half, half)]
        send(ref, ref, za_s.at[dr, k, t], za_r.at[dr, k, t], z_to[dr])

    def w_arrive(k, t):
        for dr in (0, 1):
            c = ring(-1 - k if dr == 0 else 1 + k)
            ref = w_all.at[t, c] if k < 3 else w_all.at[t, c, :, pl.ds(dr * half, half)]
            arrive(ref, za_s.at[dr, k, t], za_r.at[dr, k, t], z_to[1 - dr])
            if k < 3:
                w_send(dr, k + 1, t)

    for dr in (0, 1):
        w_send(dr, 0, 0)

    ids = ids_ref[...]
    probs = probs_ref[...]
    want = lax.broadcasted_iota(jnp.int32, (128, 128), 1) // CAP
    slot = (lax.broadcasted_iota(jnp.int32, (128, 128), 1) % CAP).astype(F32)
    hit = jnp.zeros((128, 128), F32)
    chosen = jnp.zeros((128, 128), F32)
    for k in range(ids.shape[1]):
        m = ids[:, k : k + 1] == want
        hit = hit + jnp.where(m, 1.0, 0.0)
        chosen = chosen + jnp.where(m, probs[:, k : k + 1], 0.0)
    below = jnp.where(
        lax.broadcasted_iota(jnp.int32, (128, 128), 1) < lax.broadcasted_iota(jnp.int32, (128, 128), 0),
        1.0,
        0.0,
    ).astype(BF)
    rank = jnp.dot(below, hit.astype(BF), preferred_element_type=F32)
    placed = jnp.where((hit == 1.0) & (rank == slot) & (want < 8), 1.0, 0.0)
    picker_t = placed.T[:64].astype(BF)
    prob_t = jnp.sum((placed * chosen).T[:64], axis=1, keepdims=True)
    loads[3].wait()
    rows_in = jnp.dot(picker_t, tok[...], preferred_element_type=F32)
    loads[4].wait()
    rows_cot = prob_t * jnp.dot(picker_t, cot[...], preferred_element_type=F32)
    msg[...] = jnp.concatenate(
        [rows_in.reshape(8, CAP, width), rows_cot.reshape(8, CAP, width)], axis=1
    ).astype(BF)
    for i in range(1, 8):
        send(msg.at[flip(FLIPS[i])], x_all.at[dp, e], ca_s.at[i], ca_r.at[i], c_to[i])
    x_all[dp, e] = msg[e]
    for t in (1, 2):
        for dr in (0, 1):
            w_send(dr, 0, t)

    def grp(d, j):
        return x_all.at[d, pl.ds(group(j) * 2, 2)]

    def xa_send(rel, j):
        for dr in (0, 1):
            ref = grp(dpx(rel, 0), j)
            send(ref, ref, xa_s.at[dr, rel, j], xa_r.at[dr, rel, j], x_to[dr])

    def cell_group(j):
        for fc in (0, 1):
            i = j * 2 + fc
            if i:
                ref = x_all.at[dp, flip(FLIPS[i])]
                arrive(ref, ca_s.at[i], ca_r.at[i], c_to[i])
        xa_send(0, j)
        ref = grp(dp, j)
        send(ref, ref, ya_s.at[j], ya_r.at[j], y_to)

    def y_group(j):
        arrive(grp(dpx(1, 0), j), ya_s.at[j], ya_r.at[j], y_to)
        xa_send(1, j)

    def xa_arrive(dr, rel, j):
        arrive(grp(dpx(rel, -1 if dr == 0 else 1), j), xa_s.at[dr, rel, j], xa_r.at[dr, rel, j], x_to[1 - dr])

    def relay(rel, j):
        dr = j // 2
        xa_arrive(dr, rel, j)
        ref = grp(dpx(rel, -1 if dr == 0 else 1), j)
        send(ref, ref, xb_s.at[rel, j], xb_r.at[rel, j], x_to[dr])

    def xb_arrive(rel, j):
        dr = j // 2
        arrive(grp(dpx(rel, 2), j), xb_s.at[rel, j], xb_r.at[rel, j], x_to[1 - dr])

    cell_group(0)
    w_arrive(0, 0)
    cell_group(1)
    cell_group(2)
    w_arrive(0, 1)
    cell_group(3)
    w_arrive(0, 2)
    relay(0, 0)
    y_group(0)
    w_arrive(1, 0)
    relay(0, 1)
    y_group(1)
    w_arrive(1, 1)
    relay(0, 2)
    y_group(2)
    w_arrive(1, 2)
    relay(0, 3)
    y_group(3)
    w_arrive(2, 0)
    relay(1, 0)
    w_arrive(2, 1)
    relay(1, 1)
    w_arrive(2, 2)
    relay(1, 2)
    relay(1, 3)
    for t in (0, 1, 2):
        w_arrive(3, t)
    for rel in (0, 1):
        for j in range(4):
            xa_arrive(1 - j // 2, rel, j)
            xb_arrive(rel, j)

    for i in range(4):
        rows = x_all[2 * i : 2 * i + 2].reshape(256, width)
        first = lax.dot_general(
            rows, w_all[...].reshape(384, width), (((1,), (1,)), ((), ())), preferred_element_type=F32
        ).reshape(16, 2, CAP, 384)
        pre = first[:, 0, :, 0:128]
        upward = first[:, 0, :, 128:256]
        dhidden = first[:, 1, :, 256:384]
        sigmoid = jax.nn.sigmoid(pre)
        swish = pre * sigmoid
        slope = sigmoid * (1.0 + pre * (1.0 - sigmoid))
        active = swish * upward
        dgate = dhidden * upward * slope
        dupward = dhidden * swish
        zero = jnp.zeros_like(active)
        top = jnp.concatenate([dgate, dupward, zero], axis=2)
        low = jnp.concatenate([zero, zero, active], axis=2)
        both = jnp.concatenate([top[:, None], low[:, None]], axis=1).reshape(256, 384)
        lt[:, i * 256 : (i + 1) * 256] = both.T.astype(BF)
        pair[i * 128 : (i + 1) * 128, :] = top.reshape(128, 384)[:, :256].astype(BF)

    tile = 256

    def grad_tile(n, carry):
        cols = pl.ds(pl.multiple_of(n * tile, tile), tile)
        g = jnp.dot(lt[...], x_all[:, :, :, cols].reshape(1024, tile), preferred_element_type=F32)
        grad[:, :, :, cols] = g.reshape(3, 8, 16, tile)
        return carry

    lax.fori_loop(0, width // tile, grad_tile, 0)

    def zg_refs(dr, k, t):
        if k == 0:
            cols = pl.ds(dr * half, half)
            return zs.at[dr, k, t, :, cols], zr.at[dr, k, t, :, cols]
        return zs.at[dr, k, t], zr.at[dr, k, t]

    def zg_send(dr, k, t):
        src, dst = zg_refs(dr, k, t)
        send(src, dst, zg_s.at[dr, k, t], zg_r.at[dr, k, t], z_to[dr])

    def zg_arrive(dr, k, t):
        arrive(zg_refs(dr, k, t)[1], zg_s.at[dr, k, t], zg_r.at[dr, k, t], z_to[1 - dr])

    for t in range(3):
        for dr in (0, 1):
            zs[dr, 0, t, :, dr * half : (dr + 1) * half] = grad[
                t, ring(4), :, dr * half : (dr + 1) * half
            ].astype(BF)
            zg_send(dr, 0, t)

    def zg_step(k, t):
        for dr in (0, 1):
            zg_arrive(dr, k - 1, t)
            c = ring((4 - k) if dr == 0 else (k - 4))
            if k == 1:
                a, b = dr * half, (dr + 1) * half
                oa, ob = (1 - dr) * half, (2 - dr) * half
                zs[dr, k, t, :, a:b] = (grad[t, c, :, a:b] + zr[dr, 0, t, :, a:b].astype(F32)).astype(BF)
                zs[dr, k, t, :, oa:ob] = grad[t, c, :, oa:ob].astype(BF)
            else:
                zs[dr, k, t] = (grad[t, c] + zr[dr, k - 1, t].astype(F32)).astype(BF)
            zg_send(dr, k, t)

    def part_tile(i, carry):
        p = jnp.dot(
            pair[pl.ds(pl.multiple_of(i * 128, 128), 128), :],
            w_all[0:2].reshape(256, width),
            preferred_element_type=F32,
        )
        part[pl.ds(i * 2, 2)] = p.reshape(2, 64, width)
        return carry

    lax.fori_loop(0, 4, part_tile, 0)

    for rel in (1, 0):
        for dr in (0, 1):
            ps0[dr, rel] = part[dpx(rel, 2), dr * 32 : (dr + 1) * 32].astype(BF)
            send(ps0.at[dr, rel], pr0.at[dr, rel], p0_s.at[dr, rel], p0_r.at[dr, rel], x_to[dr])

    def p1_send(dr, rel, h):
        send(ps1.at[dr, rel, h], pr1.at[dr, rel, h], p1_s.at[dr, rel, h], p1_r.at[dr, rel, h], x_to[dr])

    for rel in (1, 0):
        for dr in (0, 1):
            h = 1 - dr
            ps1[dr, rel, h] = part[dpx(rel, 1 if dr == 0 else -1), h * 32 : (h + 1) * 32].astype(BF)
            p1_send(dr, rel, h)

    def p1_step(rel):
        for dr in (0, 1):
            arrive(pr0.at[dr, rel], p0_s.at[dr, rel], p0_r.at[dr, rel], x_to[1 - dr])
            h = dr
            mine = part[dpx(rel, 1 if dr == 0 else -1), h * 32 : (h + 1) * 32]
            ps1[dr, rel, h] = (mine + pr0[dr, rel].astype(F32)).astype(BF)
            p1_send(dr, rel, h)

    def p2_sum(rel, h):
        for dr in (0, 1):
            arrive(
                pr1.at[dr, rel, h], p1_s.at[dr, rel, h], p1_r.at[dr, rel, h], x_to[1 - dr]
            )
        return (
            part[dpx(rel, 0), h * 32 : (h + 1) * 32]
            + pr1[0, rel, h].astype(F32)
            + pr1[1, rel, h].astype(F32)
        )

    for t in range(3):
        zg_step(1, t)
    p1_step(1)
    p1_step(0)
    for t in range(3):
        zg_step(2, t)
    for h in (0, 1):
        ys[h] = p2_sum(1, h).astype(BF)
        send(ys.at[h], yr.at[h], yb_s.at[h], yb_r.at[h], y_to)
    for t in range(3):
        zg_step(3, t)
    for h in (0, 1):
        mine = p2_sum(0, h)
        arrive(yr.at[h], yb_s.at[h], yb_r.at[h], y_to)
        total = mine + yr[h].astype(F32)
        bs[h * 4 : (h + 1) * 4] = total.reshape(4, CAP, width).astype(BF)
    for i in range(1, 8):
        send(bs.at[flip(FLIPS[i])], br.at[e], cb_s.at[i], cb_r.at[i], c_to[i])
    br[e] = bs[e]

    def fg_send_x(rel, t):
        for dr in (0, 1):
            ref = fg.at[t, dpx(rel, 0)]
            send(ref, ref, xg_s.at[dr, rel, t], xg_r.at[dr, rel, t], x_to[dr])

    for t in range(3):
        zg_arrive(0, 3, t)
        zg_arrive(1, 3, t)
        fg[t, dp] = (grad[t, s] + zr[0, 3, t].astype(F32) + zr[1, 3, t].astype(F32)).astype(BF)
        ref = fg.at[t, dp]
        send(ref, ref, yg_s.at[t], yg_r.at[t], y_to)
        fg_send_x(0, t)

    for i in range(1, 8):
        arrive(br.at[flip(FLIPS[i])], cb_s.at[i], cb_r.at[i], c_to[i])
    gi_ref[...] = jnp.dot(
        placed[:, :64].astype(BF),
        br[...].astype(F32).reshape(64, width).astype(BF),
        preferred_element_type=F32,
    ).astype(BF)

    for t in range(3):
        arrive(fg.at[t, dpx(1, 0)], yg_s.at[t], yg_r.at[t], y_to)
        fg_send_x(1, t)

    def far(dr, rel, t, k):
        ref = fg.at[t, dpx(rel, k)]
        if t == 2:
            ref = fg.at[t, dpx(rel, k), :, pl.ds(dr * half, half)]
        return ref

    for rel in (0, 1):
        for t in range(3):
            for dr in (0, 1):
                k = -1 if dr == 0 else 1
                arrive(fg.at[t, dpx(rel, k)], xg_s.at[dr, rel, t], xg_r.at[dr, rel, t], x_to[1 - dr])
                if t == 2 or t == dr:
                    ref = far(dr, rel, t, k)
                    send(ref, ref, xh_s.at[dr, rel, t // 2], xh_r.at[dr, rel, t // 2], x_to[dr])
    for rel in (0, 1):
        for t in range(3):
            for dr in (0, 1):
                if t == 2 or t == dr:
                    arrive(far(dr, rel, t, 2), xh_s.at[dr, rel, t // 2], xh_r.at[dr, rel, t // 2], x_to[1 - dr])
    for c in sends:
        c.wait_send()


def local(tokens, cotangent, expert_ids, gate_probs, gate_weight, up_weight, down_weight):
    rows, width = tokens.shape
    hid = down_weight.shape[1]
    v = pl.BlockSpec(memory_space=pltpu.VMEM)
    a = pl.BlockSpec(memory_space=pl.ANY)
    vm = pltpu.VMEM
    grad_input, grads = pl.pallas_call(
        kernel,
        out_shape=(
            jax.ShapeDtypeStruct((rows, width), BF),
            jax.ShapeDtypeStruct((3, 8, 16, width), BF),
        ),
        in_specs=[v, v, a, a, a, a, a],
        out_specs=(v, v),
        scratch_shapes=[
            vm((rows, width), BF),
            vm((rows, width), BF),
            vm((width, hid), BF),
            vm((width, hid), BF),
            vm((hid, width), BF),
            vm((8, 16, width), BF),
            vm((8, 8, 16, width), BF),
            vm((3, 8, 16, width), BF),
            vm((384, 1024), BF),
            vm((512, 256), BF),
            vm((3, 8, 16, width), F32),
            vm((8, 64, width), F32),
            vm((2, 4, 3, 16, width), BF),
            vm((2, 4, 3, 16, width), BF),
            vm((2, 2, 32, width), BF),
            vm((2, 2, 32, width), BF),
            vm((2, 2, 2, 32, width), BF),
            vm((2, 2, 2, 32, width), BF),
            vm((2, 32, width), BF),
            vm((2, 32, width), BF),
            vm((8, 8, width), BF),
            vm((8, 8, width), BF),
            DMA((5,)),
            DMA((2, 4, 3)),
            DMA((2, 4, 3)),
            DMA((8,)),
            DMA((8,)),
            DMA((4,)),
            DMA((4,)),
            DMA((2, 2, 4)),
            DMA((2, 2, 4)),
            DMA((2, 4)),
            DMA((2, 4)),
            DMA((2, 4, 3)),
            DMA((2, 4, 3)),
            DMA((2, 2)),
            DMA((2, 2)),
            DMA((2, 2, 2)),
            DMA((2, 2, 2)),
            DMA((2,)),
            DMA((2,)),
            DMA((8,)),
            DMA((8,)),
            DMA((3,)),
            DMA((3,)),
            DMA((2, 2, 3)),
            DMA((2, 2, 3)),
            DMA((2, 2, 2)),
            DMA((2, 2, 2)),
        ],
        compiler_params=pltpu.CompilerParams(
            collective_id=0, has_side_effects=True, vmem_limit_bytes=60 * 1024 * 1024
        ),
    )(expert_ids, gate_probs, tokens, cotangent, gate_weight, up_weight, down_weight)
    grads = grads.reshape(3, hid, width)
    return (grad_input, grads[0].T[None], grads[1].T[None], grads[2][None])


def solution(mesh):
    tok = P(("dp", "expert"), None)
    wgt = P("expert", None, None)
    return jax.shard_map(
        local,
        mesh=mesh,
        in_specs=(tok, tok, tok, tok, wgt, wgt, wgt),
        out_specs=(tok, wgt, wgt, wgt),
        check_vma=False,
    )
```

time: 398 us -> 122 us (0.31)
  waiting for transfers between devices: 339 us -> 0 us
  Pallas kernels: 0 us -> 113 us
  blocking collectives: 22.5 us -> 0 us
  between operations: 13.9 us -> 0.64 us
  matrix products: 10.2 us -> 0 us
    all_gather x3 -> x0, waiting for transfers between devices: 191 us -> none  [the longest x1 83.7 us: local(): both = lax.all_gather(message, 'dp', axis=0)]
    reduce_scatter x2 -> x0, waiting for transfers between devices: 148 us -> none  [the longest x1 92.7 us: local(): part = lax.psum_scatter(part, 'dp', scatter_dimension=0, tiled=False)]
    pallas_call x0 -> x1, Pallas kernels: none -> 113 us  [local(): pl.pallas_call(kernel, out_shape=(jax.ShapeDtypeStruct((rows, width), BF)...]
    all_to_all x2 -> x0, blocking collectives: 22.5 us -> none  [the longest x1 13.1 us: local(): lax.all_to_all(message, 'expert', split_axis=0, concat_axis=0, axis_index...]
    dot_general x6 -> x0, matrix products: 10.2 us -> none  [the longest x1 4.74 us: local(): lax.dot_general(both, weights, (((1,), (1,)), ((), ())), preferred_elemen...]
  transfers between devices with their start and end apart: 5 -> 0, of which waited for: 5 -> 0; matrix products, arithmetic and copies ran while one was open for 1% -> 0% of each run, Pallas kernels for 0% -> 0%
where the time goes in v2:
time: 122 us
  Pallas kernels  113 us (93%)
  local copies, waits for them, and re-layouts  7.91 us (6%)
    pallas_call x1, Pallas kernels, local(): pl.pallas_call(kernel, out_shape=(jax.ShapeDtypeStruct((rows, width), BF)...  113 us
    unnamed x5, local copies, waits for them, and re-layouts  3.63 us

profile of v2, /device:TPU:6, one launch (start us, length us, event | category | flops | bytes accessed | tf_op | source)
XLA Modules:
  0.0 121.9 jit_solution(5741925461358038357)
XLA Ops:
  0.6 1.4 %copy.11.ids_ref = s32[128,8]{1,0:T(8,128)} copy(s32[128,8]{0,1:T(8,128)} %param.9) | data formatting | bytes 8192 | tf_op args[2]
  2.0 1.4 %copy.12.probs_ref = f32[128,8]{1,0:T(8,128)} copy(f32[128,8]{0,1:T(8,128)} %param.10) | data formatting | bytes 8192 | tf_op args[3]
  3.5 113.4 %shard_map.102 = (bf16[128,2048]{1,0:T(8,128)(2,1)}, bf16[3,8,16,2048]{3,2,1,0:T(8,128)(2,1)}) custom-call(s32[128,8]{1,0:T(8,128)} %copy.11.ids_ref, f32[128,8]{1,0:T(8,128)} %copy.12.probs_ref, bf16[128,2048]{1,0:T(8,128)(2,1)} %tok_hbm.1, bf16[128,2048]{1,0:T(8,128)(2,1)} %cot_hbm.1, bf16[1,2048,128]{2,1,0:T(8,128)(2,1)} %gate_hbm.1, ...), custom_call_target="tpu_custom_call" | custom-call | tf_op jit(solution)/shard_map/pallas_call | solution.py:446
  116.8 2.3 %fusion = (bf16[1,8,16,2048]{3,2,1,0:T(8,128)(2,1)}, bf16[1,8,16,2048]{3,2,1,0:T(8,128)(2,1)S(1)}, bf16[1,8,16,2048]{3,2,1,0:T(8,128)(2,1)S(1)}) fusion(bf16[3,8,16,2048]{3,2,1,0:T(8,128)(2,1)} %get-tuple-element.7), kind=kLoop, calls=%fused_computation | loop fusion | bytes 3145728 | tf_op jit(solution)/shard_map/slice | solution.py:510
  119.1 0.0 copy-start
  119.1 1.0 copy.14
  120.1 1.0 copy.13
  121.1 0.0 copy-done
  121.1 0.8 copy.16
Async XLA Ops:
  119.1 2.0 %copy-start = (bf16[128,2048]{1,0:T(8,128)(2,1)S(1)}, bf16[128,2048]{1,0:T(8,128)(2,1)}, u32[]{:S(2)}) copy-start(bf16[128,2048]{1,0:T(8,128)(2,1)} %get-tuple-element.15) | copy-start | bytes 1572868

commit v3 on v2

--- a/solution.py
+++ b/solution.py
@@ -12,6 +12,7 @@
 F32 = jnp.float32
 MESH = pl.DeviceIdType.MESH
 DMA = pltpu.SemaphoreType.DMA
+ALL = [(0, 1), (0, -1), (1, 0), (0, 2), (1, 1), (1, -1), (1, 2)]
 FLIPS = [(fz, fy, fc) for fz in (0, 1) for fy in (0, 1) for fc in (0, 1)]
 
 
@@ -24,12 +25,13 @@
     up_hbm,
     down_hbm,
     gi_ref,
-    fg,
+    gg_ref,
+    gu_ref,
+    gd_ref,
     tok,
     cot,
     gate,
     up,
-    down,
     msg,
     x_all,
     w_all,
@@ -58,6 +60,8 @@
     xa_r,
     xb_s,
     xb_r,
+    yx_s,
+    yx_r,
     zg_s,
     zg_r,
     p0_s,
@@ -74,7 +78,10 @@
     xg_r,
     xh_s,
     xh_r,
+    dg_s,
+    dg_r,
 ):
+    fg = (gg_ref, gu_ref, gd_ref)
     width = tok.shape[1]
     half = width // 2
     dp = lax.axis_index("dp")
@@ -101,6 +108,8 @@
     z_to = [(dp, ring(1) * 8 + e), (dp, ring(-1) * 8 + e)]
     x_to = [(dpx(0, 1), ex), (dpx(0, -1), ex)]
     y_to = (dpx(1, 0), ex)
+    all_to = [(dpx(rel, k), ex) for rel, k in ALL]
+    far_to = [(dpx(rel, k), ex) for rel, k in ALL[3:]]
     c_to = [(dp, s * 8 + flip(f)) for f in FLIPS]
     sends = []
 
@@ -116,33 +125,41 @@
             src_ref=dst, dst_ref=dst, send_sem=ssem, recv_sem=rsem, device_id=frm, device_id_type=MESH
         ).wait_recv()
 
+    piece = down_hbm.at[0, pl.ds(pl.multiple_of(dp * 16, 16), 16)]
     loads = [
         pltpu.make_async_copy(a, b, load_sem.at[i])
         for i, (a, b) in enumerate(
-            [(gate_hbm.at[0], gate), (up_hbm.at[0], up), (down_hbm.at[0], down), (tok_hbm, tok), (cot_hbm, cot)]
+            [(piece, w_all.at[2, s]), (tok_hbm, tok), (cot_hbm, cot), (gate_hbm.at[0], gate), (up_hbm.at[0], up)]
         )
     ]
     for c in loads:
         c.start()
 
     barrier = pltpu.get_barrier_semaphore()
-    partners = z_to + x_to + [y_to] + c_to[1:]
+    partners = z_to + x_to + [y_to] + c_to[1:] + far_to
     for to in partners:
         pl.semaphore_signal(barrier, inc=1, device_id=to, device_id_type=MESH)
 
-    row = lax.broadcasted_iota(jnp.int32, (16, 128), 0)
-    lane = lax.broadcasted_iota(jnp.int32, (16, 128), 1)
-    sel = jnp.where(lane == row + dp * 16, 1.0, 0.0).astype(BF)
-    loads[0].wait()
-    w_all[0, s] = lax.dot_general(
-        sel, gate[...], (((1,), (1,)), ((), ())), preferred_element_type=F32
+    ids = ids_ref[...]
+    probs = probs_ref[...]
+    want = lax.broadcasted_iota(jnp.int32, (64, 128), 0) // CAP
+    slot = (lax.broadcasted_iota(jnp.int32, (64, 128), 0) % CAP).astype(F32)
+    hit = jnp.zeros((64, 128), F32)
+    chosen = jnp.zeros((64, 128), F32)
+    for k in range(ids.shape[0]):
+        m = ids[k : k + 1, :] == want
+        hit = hit + jnp.where(m, 1.0, 0.0)
+        chosen = chosen + jnp.where(m, probs[k : k + 1, :], 0.0)
+    before = jnp.where(
+        lax.broadcasted_iota(jnp.int32, (128, 128), 0) < lax.broadcasted_iota(jnp.int32, (128, 128), 1),
+        1.0,
+        0.0,
     ).astype(BF)
-    loads[1].wait()
-    w_all[1, s] = lax.dot_general(
-        sel, up[...], (((1,), (1,)), ((), ())), preferred_element_type=F32
-    ).astype(BF)
-    loads[2].wait()
-    w_all[2, s] = down[pl.ds(pl.multiple_of(dp * 16, 16), 16), :]
+    rank = jnp.dot(hit.astype(BF), before, preferred_element_type=F32)
+    placed = jnp.where((hit == 1.0) & (rank == slot), 1.0, 0.0)
+    picker = placed.astype(BF)
+    prob = jnp.sum(placed * chosen, axis=1, keepdims=True)
+
     pl.semaphore_wait(barrier, len(partners))
 
     def w_send(dr, k, t):
@@ -158,111 +175,117 @@
             if k < 3:
                 w_send(dr, k + 1, t)
 
+    loads[0].wait()
     for dr in (0, 1):
-        w_send(dr, 0, 0)
-
-    ids = ids_ref[...]
-    probs = probs_ref[...]
-    want = lax.broadcasted_iota(jnp.int32, (128, 128), 1) // CAP
-    slot = (lax.broadcasted_iota(jnp.int32, (128, 128), 1) % CAP).astype(F32)
-    hit = jnp.zeros((128, 128), F32)
-    chosen = jnp.zeros((128, 128), F32)
-    for k in range(ids.shape[1]):
-        m = ids[:, k : k + 1] == want
-        hit = hit + jnp.where(m, 1.0, 0.0)
-        chosen = chosen + jnp.where(m, probs[:, k : k + 1], 0.0)
-    below = jnp.where(
-        lax.broadcasted_iota(jnp.int32, (128, 128), 1) < lax.broadcasted_iota(jnp.int32, (128, 128), 0),
-        1.0,
-        0.0,
-    ).astype(BF)
-    rank = jnp.dot(below, hit.astype(BF), preferred_element_type=F32)
-    placed = jnp.where((hit == 1.0) & (rank == slot) & (want < 8), 1.0, 0.0)
-    picker_t = placed.T[:64].astype(BF)
-    prob_t = jnp.sum((placed * chosen).T[:64], axis=1, keepdims=True)
-    loads[3].wait()
-    rows_in = jnp.dot(picker_t, tok[...], preferred_element_type=F32)
-    loads[4].wait()
-    rows_cot = prob_t * jnp.dot(picker_t, cot[...], preferred_element_type=F32)
+        w_send(dr, 0, 2)
+
+    loads[1].wait()
+    rows_in = jnp.dot(picker, tok[...], preferred_element_type=F32)
+    loads[2].wait()
+    rows_cot = prob * jnp.dot(picker, cot[...], preferred_element_type=F32)
     msg[...] = jnp.concatenate(
         [rows_in.reshape(8, CAP, width), rows_cot.reshape(8, CAP, width)], axis=1
     ).astype(BF)
     for i in range(1, 8):
         send(msg.at[flip(FLIPS[i])], x_all.at[dp, e], ca_s.at[i], ca_r.at[i], c_to[i])
     x_all[dp, e] = msg[e]
-    for t in (1, 2):
+
+    def unit(d, u):
+        first, n = [(e, 1), (flip((0, 0, 1)), 1), (group(1) * 2, 2), (group(2) * 2, 2),
+                    (flip((1, 1, 0)), 1), (flip((1, 1, 1)), 1)][u]
+        return x_all.at[d, pl.ds(first, n)]
+
+    def xa_send(rel, u):
+        for dr in (0, 1):
+            ref = unit(dpx(rel, 0), u)
+            send(ref, ref, xa_s.at[dr, rel, u], xa_r.at[dr, rel, u], x_to[dr])
+
+    def own(u):
+        for i in [(), (1,), (2, 3), (4, 5), (6,), (7,)][u]:
+            arrive(x_all.at[dp, flip(FLIPS[i])], ca_s.at[i], ca_r.at[i], c_to[i])
+        xa_send(0, u)
+        ref = unit(dp, u)
+        send(ref, ref, ya_s.at[u], ya_r.at[u], y_to)
+
+    def yx_send(u, i, k):
+        ref = unit(dpx(0, k), u)
+        send(ref, ref, yx_s.at[u, i], yx_r.at[u, i], y_to)
+
+    def y_in(u):
+        arrive(unit(dpx(1, 0), u), ya_s.at[u], ya_r.at[u], y_to)
+        if u >= 2:
+            xa_send(1, u)
+
+    def x_in(dr, rel, u):
+        k = -1 if dr == 0 else 1
+        ref = unit(dpx(rel, k), u)
+        arrive(ref, xa_s.at[dr, rel, u], xa_r.at[dr, rel, u], x_to[1 - dr])
+        if u % 2 == dr:
+            send(ref, ref, xb_s.at[rel, u], xb_r.at[rel, u], x_to[dr])
+        if u < 2:
+            yx_send(u, dr, k)
+
+    def far_in(rel, u):
+        dr = u % 2
+        arrive(unit(dpx(rel, 2), u), xb_s.at[rel, u], xb_r.at[rel, u], x_to[1 - dr])
+        if u < 2:
+            yx_send(u, 2, 2)
+
+    def yx_in(i, k):
+        for u in (0, 1):
+            arrive(unit(dpx(1, k), u), yx_s.at[u, i], yx_r.at[u, i], y_to)
+
+    own(0)
+
+    row = lax.broadcasted_iota(jnp.int32, (16, 128), 0)
+    lane = lax.broadcasted_iota(jnp.int32, (16, 128), 1)
+    sel = jnp.where(lane == row + dp * 16, 1.0, 0.0).astype(BF)
+    for t, ref in ((0, gate), (1, up)):
+        loads[3 + t].wait()
+        w_all[t, s] = lax.dot_general(
+            sel, ref[...], (((1,), (1,)), ((), ())), preferred_element_type=F32
+        ).astype(BF)
         for dr in (0, 1):
             w_send(dr, 0, t)
 
-    def grp(d, j):
-        return x_all.at[d, pl.ds(group(j) * 2, 2)]
-
-    def xa_send(rel, j):
-        for dr in (0, 1):
-            ref = grp(dpx(rel, 0), j)
-            send(ref, ref, xa_s.at[dr, rel, j], xa_r.at[dr, rel, j], x_to[dr])
-
-    def cell_group(j):
-        for fc in (0, 1):
-            i = j * 2 + fc
-            if i:
-                ref = x_all.at[dp, flip(FLIPS[i])]
-                arrive(ref, ca_s.at[i], ca_r.at[i], c_to[i])
-        xa_send(0, j)
-        ref = grp(dp, j)
-        send(ref, ref, ya_s.at[j], ya_r.at[j], y_to)
-
-    def y_group(j):
-        arrive(grp(dpx(1, 0), j), ya_s.at[j], ya_r.at[j], y_to)
-        xa_send(1, j)
-
-    def xa_arrive(dr, rel, j):
-        arrive(grp(dpx(rel, -1 if dr == 0 else 1), j), xa_s.at[dr, rel, j], xa_r.at[dr, rel, j], x_to[1 - dr])
-
-    def relay(rel, j):
-        dr = j // 2
-        xa_arrive(dr, rel, j)
-        ref = grp(dpx(rel, -1 if dr == 0 else 1), j)
-        send(ref, ref, xb_s.at[rel, j], xb_r.at[rel, j], x_to[dr])
-
-    def xb_arrive(rel, j):
-        dr = j // 2
-        arrive(grp(dpx(rel, 2), j), xb_s.at[rel, j], xb_r.at[rel, j], x_to[1 - dr])
-
-    cell_group(0)
+    own(1)
+    own(2)
+    own(3)
+    x_in(0, 0, 0)
+    w_arrive(0, 2)
+    x_in(1, 0, 1)
+    x_in(1, 0, 0)
+    x_in(0, 0, 1)
+    own(4)
+    own(5)
     w_arrive(0, 0)
-    cell_group(1)
-    cell_group(2)
+    far_in(0, 0)
+    far_in(0, 1)
     w_arrive(0, 1)
-    cell_group(3)
-    w_arrive(0, 2)
-    relay(0, 0)
-    y_group(0)
+    y_in(2)
+    x_in(0, 0, 2)
+    w_arrive(1, 2)
+    y_in(3)
+    x_in(1, 0, 3)
     w_arrive(1, 0)
-    relay(0, 1)
-    y_group(1)
+    y_in(4)
+    y_in(5)
+    x_in(0, 0, 4)
+    x_in(1, 0, 5)
     w_arrive(1, 1)
-    relay(0, 2)
-    y_group(2)
-    w_arrive(1, 2)
-    relay(0, 3)
-    y_group(3)
+    w_arrive(2, 2)
+    x_in(0, 1, 2)
     w_arrive(2, 0)
-    relay(1, 0)
+    x_in(1, 1, 3)
     w_arrive(2, 1)
-    relay(1, 1)
-    w_arrive(2, 2)
-    relay(1, 2)
-    relay(1, 3)
-    for t in (0, 1, 2):
+    x_in(0, 1, 4)
+    x_in(1, 1, 5)
+    for t in (2, 0, 1):
         w_arrive(3, t)
-    for rel in (0, 1):
-        for j in range(4):
-            xa_arrive(1 - j // 2, rel, j)
-            xb_arrive(rel, j)
-
-    for i in range(4):
-        rows = x_all[2 * i : 2 * i + 2].reshape(256, width)
+
+    def compute(k):
+        d = (dpx(0, k), dpx(1, k))
+        rows = jnp.concatenate([x_all[i].reshape(128, width) for i in d], axis=0)
         first = lax.dot_general(
             rows, w_all[...].reshape(384, width), (((1,), (1,)), ((), ())), preferred_element_type=F32
         ).reshape(16, 2, CAP, 384)
@@ -278,9 +301,27 @@
         zero = jnp.zeros_like(active)
         top = jnp.concatenate([dgate, dupward, zero], axis=2)
         low = jnp.concatenate([zero, zero, active], axis=2)
-        both = jnp.concatenate([top[:, None], low[:, None]], axis=1).reshape(256, 384)
-        lt[:, i * 256 : (i + 1) * 256] = both.T.astype(BF)
-        pair[i * 128 : (i + 1) * 128, :] = top.reshape(128, 384)[:, :256].astype(BF)
+        both = jnp.concatenate([top[:, None], low[:, None]], axis=1).reshape(256, 384).T.astype(BF)
+        pairs = top.reshape(128, 384)[:, :256].astype(BF)
+        for i in (0, 1):
+            lt[:, pl.ds(pl.multiple_of(d[i] * 128, 128), 128)] = both[:, i * 128 : (i + 1) * 128]
+            pair[pl.ds(pl.multiple_of(d[i] * 64, 64), 64), :] = pairs[i * 64 : (i + 1) * 64]
+
+    y_in(0)
+    y_in(1)
+    compute(0)
+    for dr in (0, 1):
+        for rel in (0, 1):
+            for u in (2, 3, 4, 5):
+                if u % 2 != dr:
+                    x_in(dr, rel, u)
+        yx_in(dr, -1 if dr == 0 else 1)
+        compute(-1 if dr == 0 else 1)
+    for rel in (0, 1):
+        for u in (2, 3, 4, 5):
+            far_in(rel, u)
+    yx_in(2, 2)
+    compute(2)
 
     tile = 256
 
@@ -290,8 +331,6 @@
         grad[:, :, :, cols] = g.reshape(3, 8, 16, tile)
         return carry
 
-    lax.fori_loop(0, width // tile, grad_tile, 0)
-
     def zg_refs(dr, k, t):
         if k == 0:
             cols = pl.ds(dr * half, half)
@@ -305,8 +344,10 @@
     def zg_arrive(dr, k, t):
         arrive(zg_refs(dr, k, t)[1], zg_s.at[dr, k, t], zg_r.at[dr, k, t], z_to[1 - dr])
 
-    for t in range(3):
-        for dr in (0, 1):
+    steps = width // tile // 2
+    for dr in (0, 1):
+        lax.fori_loop(dr * steps, (dr + 1) * steps, grad_tile, 0)
+        for t in range(3):
             zs[dr, 0, t, :, dr * half : (dr + 1) * half] = grad[
                 t, ring(4), :, dr * half : (dr + 1) * half
             ].astype(BF)
@@ -391,48 +432,46 @@
 
     def fg_send_x(rel, t):
         for dr in (0, 1):
-            ref = fg.at[t, dpx(rel, 0)]
+            ref = fg[t].at[dpx(rel, 0)]
             send(ref, ref, xg_s.at[dr, rel, t], xg_r.at[dr, rel, t], x_to[dr])
 
     for t in range(3):
         zg_arrive(0, 3, t)
         zg_arrive(1, 3, t)
-        fg[t, dp] = (grad[t, s] + zr[0, 3, t].astype(F32) + zr[1, 3, t].astype(F32)).astype(BF)
-        ref = fg.at[t, dp]
-        send(ref, ref, yg_s.at[t], yg_r.at[t], y_to)
-        fg_send_x(0, t)
+        fg[t][dp] = (grad[t, s] + zr[0, 3, t].astype(F32) + zr[1, 3, t].astype(F32)).astype(BF)
+        ref = fg[t].at[dp]
+        if t < 2:
+            send(ref, ref, yg_s.at[t], yg_r.at[t], y_to)
+            fg_send_x(0, t)
+        else:
+            for i, to in enumerate(all_to):
+                send(ref, ref, dg_s.at[i], dg_r.at[i], to)
 
     for i in range(1, 8):
         arrive(br.at[flip(FLIPS[i])], cb_s.at[i], cb_r.at[i], c_to[i])
-    gi_ref[...] = jnp.dot(
-        placed[:, :64].astype(BF),
+    gi_ref[...] = lax.dot_general(
+        picker,
         br[...].astype(F32).reshape(64, width).astype(BF),
+        (((0,), (0,)), ((), ())),
         preferred_element_type=F32,
     ).astype(BF)
 
-    for t in range(3):
-        arrive(fg.at[t, dpx(1, 0)], yg_s.at[t], yg_r.at[t], y_to)
+    for t in (0, 1):
+        arrive(fg[t].at[dpx(1, 0)], yg_s.at[t], yg_r.at[t], y_to)
         fg_send_x(1, t)
-
-    def far(dr, rel, t, k):
-        ref = fg.at[t, dpx(rel, k)]
-        if t == 2:
-            ref = fg.at[t, dpx(rel, k), :, pl.ds(dr * half, half)]
-        return ref
-
     for rel in (0, 1):
-        for t in range(3):
+        for t in (0, 1):
             for dr in (0, 1):
                 k = -1 if dr == 0 else 1
-                arrive(fg.at[t, dpx(rel, k)], xg_s.at[dr, rel, t], xg_r.at[dr, rel, t], x_to[1 - dr])
-                if t == 2 or t == dr:
-                    ref = far(dr, rel, t, k)
-                    send(ref, ref, xh_s.at[dr, rel, t // 2], xh_r.at[dr, rel, t // 2], x_to[dr])
+                ref = fg[t].at[dpx(rel, k)]
+                arrive(ref, xg_s.at[dr, rel, t], xg_r.at[dr, rel, t], x_to[1 - dr])
+                if t == dr:
+                    send(ref, ref, xh_s.at[rel, t], xh_r.at[rel, t], x_to[dr])
     for rel in (0, 1):
-        for t in range(3):
-            for dr in (0, 1):
-                if t == 2 or t == dr:
-                    arrive(far(dr, rel, t, 2), xh_s.at[dr, rel, t // 2], xh_r.at[dr, rel, t // 2], x_to[1 - dr])
+        for t in (0, 1):
+            arrive(fg[t].at[dpx(rel, 2)], xh_s.at[rel, t], xh_r.at[rel, t], x_to[1 - t])
+    for i, (rel, k) in enumerate(ALL):
+        arrive(fg[2].at[dpx(rel, -k)], dg_s.at[i], dg_r.at[i], (dpx(rel, -k), ex))
     for c in sends:
         c.wait_send()
 
@@ -443,20 +482,22 @@
     v = pl.BlockSpec(memory_space=pltpu.VMEM)
     a = pl.BlockSpec(memory_space=pl.ANY)
     vm = pltpu.VMEM
-    grad_input, grads = pl.pallas_call(
+    grad = jax.ShapeDtypeStruct((8, 16, width), BF)
+    grad_input, *grads = pl.pallas_call(
         kernel,
         out_shape=(
             jax.ShapeDtypeStruct((rows, width), BF),
-            jax.ShapeDtypeStruct((3, 8, 16, width), BF),
+            grad,
+            grad,
+            grad,
         ),
         in_specs=[v, v, a, a, a, a, a],
-        out_specs=(v, v),
+        out_specs=(v, v, v, v),
         scratch_shapes=[
             vm((rows, width), BF),
             vm((rows, width), BF),
             vm((width, hid), BF),
             vm((width, hid), BF),
-            vm((hid, width), BF),
             vm((8, 16, width), BF),
             vm((8, 8, 16, width), BF),
             vm((3, 8, 16, width), BF),
@@ -479,12 +520,14 @@
             DMA((2, 4, 3)),
             DMA((8,)),
             DMA((8,)),
-            DMA((4,)),
-            DMA((4,)),
-            DMA((2, 2, 4)),
-            DMA((2, 2, 4)),
-            DMA((2, 4)),
-            DMA((2, 4)),
+            DMA((6,)),
+            DMA((6,)),
+            DMA((2, 2, 6)),
+            DMA((2, 2, 6)),
+            DMA((2, 6)),
+            DMA((2, 6)),
+            DMA((2, 3)),
+            DMA((2, 3)),
             DMA((2, 4, 3)),
             DMA((2, 4, 3)),
             DMA((2, 2)),
@@ -499,14 +542,16 @@
             DMA((3,)),
             DMA((2, 2, 3)),
             DMA((2, 2, 3)),
-            DMA((2, 2, 2)),
-            DMA((2, 2, 2)),
+            DMA((2, 2)),
+            DMA((2, 2)),
+            DMA((7,)),
+            DMA((7,)),
         ],
         compiler_params=pltpu.CompilerParams(
             collective_id=0, has_side_effects=True, vmem_limit_bytes=60 * 1024 * 1024
         ),
-    )(expert_ids, gate_probs, tokens, cotangent, gate_weight, up_weight, down_weight)
-    grads = grads.reshape(3, hid, width)
+    )(expert_ids.T, gate_probs.T, tokens, cotangent, gate_weight, up_weight, down_weight)
+    grads = [g.reshape(hid, width) for g in grads]
     return (grad_input, grads[0].T[None], grads[1].T[None], grads[2][None])
 
 

time: 122 us -> 115 us (0.943)
  Pallas kernels: 113 us -> 109 us
  local copies, waits for them, and re-layouts: 7.91 us -> 5.17 us
    pallas_call x1, Pallas kernels: 113 us -> 109 us  [local(): pl.pallas_call(kernel, out_shape=(jax.ShapeDtypeStruct((rows, width), BF)...]
    reshape x0 -> x2, local copies, waits for them, and re-layouts: none -> 3.1 us  [local(): grads = [g.reshape(hid, width) for g in grads]]
    slice x1 -> x0, local copies, waits for them, and re-layouts: 2.28 us -> none  [local(): return (grad_input, grads[0].T[None], grads[1].T[None], grads[2][None])]
    squeeze x2 -> x0, local copies, waits for them, and re-layouts: 2 us -> none  [local(): return (grad_input, grads[0].T[None], grads[1].T[None], grads[2][None])]
    unnamed x5 -> x8, local copies, waits for them, and re-layouts: 3.63 us -> 2.07 us
where the time goes in v3:
time: 115 us
  Pallas kernels  109 us (95%)
  local copies, waits for them, and re-layouts  5.17 us (4%)
    pallas_call x1, Pallas kernels, local(): pl.pallas_call(kernel, out_shape=(jax.ShapeDtypeStruct((rows, width), BF)...  109 us
    reshape x2, local copies, waits for them, and re-layouts, local(): grads = [g.reshape(hid, width) for g in grads]  3.1 us

profile of v3, /device:TPU:6, one launch (start us, length us, event | category | flops | bytes accessed | tf_op | source)
XLA Modules:
  0.0 114.8 jit_solution(12026350654929745286)
XLA Ops:
  0.6 109.0 %shard_map.102 = (bf16[128,2048]{1,0:T(8,128)(2,1)}, bf16[8,16,2048]{2,1,0:T(8,128)(2,1)}, bf16[8,16,2048]{2,1,0:T(8,128)(2,1)}, bf16[8,16,2048]{2,1,0:T(8,128)(2,1)}) custom-call(s32[8,128]{1,0:T(8,128)} %bitcast.16, f32[8,128]{1,0:T(8,128)} %bitcast.17, bf16[128,2048]{1,0:T(8,128)(2,1)} %tok_hbm.1, bf16[128,2048]{1,0:T(8,128)(2,1)} %cot_hbm.1, ...), custom_call_target="tpu_custom_call" | custom-call | tf_op jit(solution)/shard_map/pallas_call | solution.py:486
  109.6 0.0 copy-start.2
  109.7 2.1 %copy.11 = bf16[128,2048]{0,1:T(8,128)(2,1)} copy(bf16[128,2048]{1,0:T(8,128)(2,1)} %bitcast.15) | data formatting | bytes 1048576 | tf_op jit(solution)/shard_map/reshape | solution.py:554
  111.8 0.0 copy-done.2
  111.8 0.0 copy-start.1
  111.8 1.0 copy.12
  112.8 0.0 copy-done.1
  112.8 0.0 copy-start
  112.8 0.8 copy.15
  113.6 0.4 copy-done
  114.0 0.8 copy.16
Async XLA Ops:
  109.6 2.1 %copy-start.2 = (bf16[8,16,2048]{2,1,0:T(8,128)(2,1)S(1)}, bf16[8,16,2048]{2,1,0:T(8,128)(2,1)}, u32[]{:S(2)}) copy-start(bf16[8,16,2048]{2,1,0:T(8,128)(2,1)} %get-tuple-element.10) | copy-start | bytes 1572868
  111.8 1.0 copy-start.1
  112.8 1.2 %copy-start = (bf16[8,16,2048]{2,1,0:T(8,128)(2,1)S(1)}, bf16[8,16,2048]{2,1,0:T(8,128)(2,1)}, u32[]{:S(2)}) copy-start(bf16[8,16,2048]{2,1,0:T(8,128)(2,1)} %get-tuple-element.11) | copy-start | bytes 1572868

commit v4 on v3

--- a/solution.py
+++ b/solution.py
@@ -331,40 +331,30 @@
         grad[:, :, :, cols] = g.reshape(3, 8, 16, tile)
         return carry
 
-    def zg_refs(dr, k, t):
-        if k == 0:
-            cols = pl.ds(dr * half, half)
-            return zs.at[dr, k, t, :, cols], zr.at[dr, k, t, :, cols]
-        return zs.at[dr, k, t], zr.at[dr, k, t]
-
-    def zg_send(dr, k, t):
-        src, dst = zg_refs(dr, k, t)
-        send(src, dst, zg_s.at[dr, k, t], zg_r.at[dr, k, t], z_to[dr])
-
-    def zg_arrive(dr, k, t):
-        arrive(zg_refs(dr, k, t)[1], zg_s.at[dr, k, t], zg_r.at[dr, k, t], z_to[1 - dr])
+    def zg_refs(dr, k, t, c):
+        cols = pl.ds(c * half, half)
+        return zs.at[dr, k, t, :, cols], zr.at[dr, k, t, :, cols]
+
+    def zg_arrive(dr, k, t, c):
+        arrive(zg_refs(dr, k, t, c)[1], zg_s.at[dr, k, t, c], zg_r.at[dr, k, t, c], z_to[1 - dr])
+
+    def zg(dr, k, t, c, add):
+        a, b = c * half, (c + 1) * half
+        value = grad[t, ring((4 - k) if dr == 0 else (k - 4)), :, a:b]
+        if add:
+            zg_arrive(dr, k - 1, t, c)
+            value = value + zr[dr, k - 1, t, :, a:b].astype(F32)
+        zs[dr, k, t, :, a:b] = value.astype(BF)
+        src, dst = zg_refs(dr, k, t, c)
+        send(src, dst, zg_s.at[dr, k, t, c], zg_r.at[dr, k, t, c], z_to[dr])
 
     steps = width // tile // 2
-    for dr in (0, 1):
-        lax.fori_loop(dr * steps, (dr + 1) * steps, grad_tile, 0)
+    for c in (0, 1):
+        lax.fori_loop(c * steps, (c + 1) * steps, grad_tile, 0)
         for t in range(3):
-            zs[dr, 0, t, :, dr * half : (dr + 1) * half] = grad[
-                t, ring(4), :, dr * half : (dr + 1) * half
-            ].astype(BF)
-            zg_send(dr, 0, t)
-
-    def zg_step(k, t):
-        for dr in (0, 1):
-            zg_arrive(dr, k - 1, t)
-            c = ring((4 - k) if dr == 0 else (k - 4))
-            if k == 1:
-                a, b = dr * half, (dr + 1) * half
-                oa, ob = (1 - dr) * half, (2 - dr) * half
-                zs[dr, k, t, :, a:b] = (grad[t, c, :, a:b] + zr[dr, 0, t, :, a:b].astype(F32)).astype(BF)
-                zs[dr, k, t, :, oa:ob] = grad[t, c, :, oa:ob].astype(BF)
-            else:
-                zs[dr, k, t] = (grad[t, c] + zr[dr, k - 1, t].astype(F32)).astype(BF)
-            zg_send(dr, k, t)
+            zg(c, 0, t, c, False)
+        for t in range(3):
+            zg(1 - c, 1, t, c, False)
 
     def part_tile(i, carry):
         p = jnp.dot(
@@ -411,16 +401,22 @@
         )
 
     for t in range(3):
-        zg_step(1, t)
+        for dr in (0, 1):
+            zg(dr, 1, t, dr, True)
     p1_step(1)
+
+    def zg_all(k, c):
+        for t in range(3):
+            for dr in (0, 1):
+                zg(dr, k, t, c, True)
+
+    zg_all(2, 1)
     p1_step(0)
-    for t in range(3):
-        zg_step(2, t)
+    zg_all(2, 0)
     for h in (0, 1):
         ys[h] = p2_sum(1, h).astype(BF)
         send(ys.at[h], yr.at[h], yb_s.at[h], yb_r.at[h], y_to)
-    for t in range(3):
-        zg_step(3, t)
+    zg_all(3, 1)
     for h in (0, 1):
         mine = p2_sum(0, h)
         arrive(yr.at[h], yb_s.at[h], yb_r.at[h], y_to)
@@ -429,23 +425,30 @@
     for i in range(1, 8):
         send(bs.at[flip(FLIPS[i])], br.at[e], cb_s.at[i], cb_r.at[i], c_to[i])
     br[e] = bs[e]
+    zg_all(3, 0)
+
+    def final(t, c):
+        a, b = c * half, (c + 1) * half
+        for dr in (0, 1):
+            zg_arrive(dr, 3, t, c)
+        total = grad[t, s, :, a:b]
+        for dr in (0, 1):
+            total = total + zr[dr, 3, t, :, a:b].astype(F32)
+        fg[t][dp, :, a:b] = total.astype(BF)
+
+    def late(t, rel, k):
+        return fg[t].at[dpx(rel, k), :, pl.ds(half, half)]
 
     def fg_send_x(rel, t):
         for dr in (0, 1):
-            ref = fg[t].at[dpx(rel, 0)]
+            ref = late(t, rel, 0)
             send(ref, ref, xg_s.at[dr, rel, t], xg_r.at[dr, rel, t], x_to[dr])
 
     for t in range(3):
-        zg_arrive(0, 3, t)
-        zg_arrive(1, 3, t)
-        fg[t][dp] = (grad[t, s] + zr[0, 3, t].astype(F32) + zr[1, 3, t].astype(F32)).astype(BF)
-        ref = fg[t].at[dp]
-        if t < 2:
-            send(ref, ref, yg_s.at[t], yg_r.at[t], y_to)
-            fg_send_x(0, t)
-        else:
-            for i, to in enumerate(all_to):
-                send(ref, ref, dg_s.at[i], dg_r.at[i], to)
+        final(t, 1)
+        ref = late(t, 0, 0)
+        send(ref, ref, yg_s.at[t], yg_r.at[t], y_to)
+        fg_send_x(0, t)
 
     for i in range(1, 8):
         arrive(br.at[flip(FLIPS[i])], cb_s.at[i], cb_r.at[i], c_to[i])
@@ -456,24 +459,60 @@
         preferred_element_type=F32,
     ).astype(BF)
 
-    for t in (0, 1):
-        arrive(fg[t].at[dpx(1, 0)], yg_s.at[t], yg_r.at[t], y_to)
+    for t in range(3):
+        arrive(late(t, 1, 0), yg_s.at[t], yg_r.at[t], y_to)
         fg_send_x(1, t)
+    for t in range(3):
+        final(t, 0)
+        ref = fg[t].at[dp, :, pl.ds(0, half)]
+        for i, to in enumerate(all_to):
+            send(ref, ref, dg_s.at[t, i], dg_r.at[t, i], to)
+
+    def relayed(t, rel, k, dr):
+        if t < 2:
+            return late(t, rel, k), t
+        return fg[t].at[dpx(rel, k), :, pl.ds(half + dr * (half // 2), half // 2)], 2 + dr
+
     for rel in (0, 1):
-        for t in (0, 1):
+        for t in range(3):
             for dr in (0, 1):
                 k = -1 if dr == 0 else 1
-                ref = fg[t].at[dpx(rel, k)]
-                arrive(ref, xg_s.at[dr, rel, t], xg_r.at[dr, rel, t], x_to[1 - dr])
-                if t == dr:
-                    send(ref, ref, xh_s.at[rel, t], xh_r.at[rel, t], x_to[dr])
+                arrive(late(t, rel, k), xg_s.at[dr, rel, t], xg_r.at[dr, rel, t], x_to[1 - dr])
+                if t == 2 or t == dr:
+                    ref, i = relayed(t, rel, k, dr)
+                    send(ref, ref, xh_s.at[rel, i], xh_r.at[rel, i], x_to[dr])
     for rel in (0, 1):
-        for t in (0, 1):
-            arrive(fg[t].at[dpx(rel, 2)], xh_s.at[rel, t], xh_r.at[rel, t], x_to[1 - t])
-    for i, (rel, k) in enumerate(ALL):
-        arrive(fg[2].at[dpx(rel, -k)], dg_s.at[i], dg_r.at[i], (dpx(rel, -k), ex))
+        for t in range(3):
+            for dr in (0, 1):
+                if t == 2 or t == dr:
+                    ref, i = relayed(t, rel, 2, dr)
+                    arrive(ref, xh_s.at[rel, i], xh_r.at[rel, i], x_to[1 - dr])
+    for t in range(3):
+        for i, (rel, k) in enumerate(ALL):
+            arrive(
+                fg[t].at[dpx(rel, -k), :, pl.ds(0, half)], dg_s.at[t, i], dg_r.at[t, i], (dpx(rel, -k), ex)
+            )
     for c in sends:
         c.wait_send()
+
+
+def finish(gi, gg, gu, gd, gi_out, gg_out, gu_out, gd_out, inner, turned, in_sem, out_sem):
+    refs = [(gg, gg_out), (gu, gu_out), (gi, gi_out), (gd, gd_out)]
+    ins = [pltpu.make_async_copy(a, inner.at[i], in_sem.at[i]) for i, (a, _) in enumerate(refs)]
+    for c in ins:
+        c.start()
+    outs = []
+    for i, (_, b) in enumerate(refs):
+        ins[i].wait()
+        src = inner.at[i]
+        if i < 2:
+            turned[i] = inner[i].T
+            src = turned.at[i]
+        c = pltpu.make_async_copy(src, b, out_sem.at[i])
+        c.start()
+        outs.append(c)
+    for c in outs:
+        c.wait()
 
 
 def local(tokens, cotangent, expert_ids, gate_probs, gate_weight, up_weight, down_weight):
@@ -528,8 +567,8 @@
             DMA((2, 6)),
             DMA((2, 3)),
             DMA((2, 3)),
-            DMA((2, 4, 3)),
-            DMA((2, 4, 3)),
+            DMA((2, 4, 3, 2)),
+            DMA((2, 4, 3, 2)),
             DMA((2, 2)),
             DMA((2, 2)),
             DMA((2, 2, 2)),
@@ -542,17 +581,32 @@
             DMA((3,)),
             DMA((2, 2, 3)),
             DMA((2, 2, 3)),
-            DMA((2, 2)),
-            DMA((2, 2)),
-            DMA((7,)),
-            DMA((7,)),
+            DMA((2, 4)),
+            DMA((2, 4)),
+            DMA((3, 7)),
+            DMA((3, 7)),
         ],
         compiler_params=pltpu.CompilerParams(
             collective_id=0, has_side_effects=True, vmem_limit_bytes=60 * 1024 * 1024
         ),
     )(expert_ids.T, gate_probs.T, tokens, cotangent, gate_weight, up_weight, down_weight)
+    flat = jax.ShapeDtypeStruct((hid, width), BF)
+    tall = jax.ShapeDtypeStruct((width, hid), BF)
     grads = [g.reshape(hid, width) for g in grads]
-    return (grad_input, grads[0].T[None], grads[1].T[None], grads[2][None])
+    grad_input, gate, up, down = pl.pallas_call(
+        finish,
+        out_shape=(flat, tall, tall, flat),
+        in_specs=[a] * 4,
+        out_specs=(a, a, a, a),
+        scratch_shapes=[
+            vm((4, hid, width), BF),
+            vm((2, width, hid), BF),
+            DMA((4,)),
+            DMA((4,)),
+        ],
+        compiler_params=pltpu.CompilerParams(vmem_limit_bytes=60 * 1024 * 1024),
+    )(grad_input, *grads)
+    return (grad_input, gate[None], up[None], down[None])
 
 
 def solution(mesh):

time: 115 us -> 117 us (1.017)
  the two profiles are of different devices: /device:TPU:6 before, /device:TPU:1 now
where the time goes in v4:
time: 117 us; the launch traced here: 116 us
  Pallas kernels  116 us (99%)
    pallas_call x1, Pallas kernels, local(): pl.pallas_call(kernel, out_shape=(jax.ShapeDtypeStruct((rows, width), BF)...  113 us
    pallas_call x1, Pallas kernels, local(): pl.pallas_call(finish, out_shape=(flat, tall, tall, flat), in_specs=[a] *...  2.63 us

profile of v4, /device:TPU:1, one launch (start us, length us, event | category | flops | bytes accessed | tf_op | source)
XLA Modules:
  0.0 116.4 jit_solution(14773460216773511842)
XLA Ops:
  0.6 113.1 %shard_map.102 = (bf16[128,2048]{1,0:T(8,128)(2,1)}, bf16[8,16,2048]{2,1,0:T(8,128)(2,1)}, bf16[8,16,2048]{2,1,0:T(8,128)(2,1)}, bf16[8,16,2048]{2,1,0:T(8,128)(2,1)}) custom-call(s32[8,128]{1,0:T(8,128)} %bitcast.11, f32[8,128]{1,0:T(8,128)} %bitcast.12, bf16[128,2048]{1,0:T(8,128)(2,1)} %tok_hbm.1, bf16[128,2048]{1,0:T(8,128)(2,1)} %cot_hbm.1, ...), custom_call_target="tpu_custom_call" | custom-call | tf_op jit(solution)/shard_map/pallas_call | solution.py:525
  113.8 2.6 %shard_map.103 = (bf16[128,2048]{1,0:T(8,128)(2,1)}, bf16[2048,128]{1,0:T(8,128)(2,1)}, bf16[2048,128]{1,0:T(8,128)(2,1)}, bf16[128,2048]{1,0:T(8,128)(2,1)}) custom-call(bf16[128,2048]{1,0:T(8,128)(2,1)} %get-tuple-element.12.gi, bf16[128,2048]{1,0:T(8,128)(2,1)} %bitcast.8, bf16[128,2048]{1,0:T(8,128)(2,1)} %bitcast.9, bf16[128,2048]{1,0:T(8,128)(2,1)} %bitcast.10), custom_call_target="tpu_custom_call" | custom-call | tf_op jit(solution)/shard_map/pallas_call | solution.py:596

commit v5 on v4

--- a/solution.py
+++ b/solution.py
@@ -17,8 +17,8 @@
 
 
 def kernel(
-    ids_ref,
-    probs_ref,
+    ids_hbm,
+    probs_hbm,
     tok_hbm,
     cot_hbm,
     gate_hbm,
@@ -28,6 +28,8 @@
     gg_ref,
     gu_ref,
     gd_ref,
+    ids_ref,
+    probs_ref,
     tok,
     cot,
     gate,
@@ -125,21 +127,24 @@
             src_ref=dst, dst_ref=dst, send_sem=ssem, recv_sem=rsem, device_id=frm, device_id_type=MESH
         ).wait_recv()
 
+    barrier = pltpu.get_barrier_semaphore()
+    partners = z_to + x_to + [y_to] + c_to[1:] + far_to
+    for to in partners:
+        pl.semaphore_signal(barrier, inc=1, device_id=to, device_id_type=MESH)
+
     piece = down_hbm.at[0, pl.ds(pl.multiple_of(dp * 16, 16), 16)]
     loads = [
         pltpu.make_async_copy(a, b, load_sem.at[i])
         for i, (a, b) in enumerate(
-            [(piece, w_all.at[2, s]), (tok_hbm, tok), (cot_hbm, cot), (gate_hbm.at[0], gate), (up_hbm.at[0], up)]
+            [(piece, w_all.at[2, s]), (tok_hbm, tok), (cot_hbm, cot), (gate_hbm.at[0], gate),
+             (up_hbm.at[0], up), (ids_hbm, ids_ref), (probs_hbm, probs_ref)]
         )
     ]
-    for c in loads:
-        c.start()
-
-    barrier = pltpu.get_barrier_semaphore()
-    partners = z_to + x_to + [y_to] + c_to[1:] + far_to
-    for to in partners:
-        pl.semaphore_signal(barrier, inc=1, device_id=to, device_id_type=MESH)
-
+    for i in (5, 6, 0, 1, 2, 3, 4):
+        loads[i].start()
+
+    loads[5].wait()
+    loads[6].wait()
     ids = ids_ref[...]
     probs = probs_ref[...]
     want = lax.broadcasted_iota(jnp.int32, (64, 128), 0) // CAP
@@ -247,8 +252,9 @@
         ).astype(BF)
         for dr in (0, 1):
             w_send(dr, 0, t)
-
-    own(1)
+        if t == 0:
+            own(1)
+
     own(2)
     own(3)
     x_in(0, 0, 0)
@@ -400,23 +406,65 @@
             + pr1[1, rel, h].astype(F32)
         )
 
-    for t in range(3):
-        for dr in (0, 1):
-            zg(dr, 1, t, dr, True)
+    def zg_all(k, c):
+        for dr in (0, 1):
+            for t in range(3):
+                zg(dr, k, t, dr if c is None else c, True)
+
+    zg_all(1, None)
     p1_step(1)
-
-    def zg_all(k, c):
-        for t in range(3):
-            for dr in (0, 1):
-                zg(dr, k, t, c, True)
-
     zg_all(2, 1)
     p1_step(0)
     zg_all(2, 0)
+    zg_all(3, 1)
     for h in (0, 1):
         ys[h] = p2_sum(1, h).astype(BF)
         send(ys.at[h], yr.at[h], yb_s.at[h], yb_r.at[h], y_to)
-    zg_all(3, 1)
+    zg_all(3, 0)
+
+    def final(t, c):
+        a, b = c * half, (c + 1) * half
+        for dr in (0, 1):
+            zg_arrive(dr, 3, t, c)
+        total = grad[t, s, :, a:b]
+        for dr in (0, 1):
+            total = total + zr[dr, 3, t, :, a:b].astype(F32)
+        fg[t][dp, :, a:b] = total.astype(BF)
+
+    order = [(0, 1), (1, 1), (2, 1), (0, 0), (1, 0), (2, 0)]
+
+    def fg_piece(p, rel, k):
+        t, c = order[p]
+        return fg[t].at[dpx(rel, k), :, pl.ds(c * half, half)]
+
+    def fg_send_x(p, rel):
+        for dr in (0, 1):
+            ref = fg_piece(p, rel, 0)
+            send(ref, ref, xg_s.at[dr, rel, p], xg_r.at[dr, rel, p], x_to[dr])
+
+    def fg_own(p):
+        final(*order[p])
+        ref = fg_piece(p, 0, 0)
+        if p < 5:
+            send(ref, ref, yg_s.at[p], yg_r.at[p], y_to)
+            fg_send_x(p, 0)
+        else:
+            for i, to in enumerate(all_to):
+                send(ref, ref, dg_s.at[i], dg_r.at[i], to)
+
+    def fg_y(p):
+        arrive(fg_piece(p, 1, 0), yg_s.at[p], yg_r.at[p], y_to)
+        fg_send_x(p, 1)
+
+    def fg_x(p, rel):
+        for dr in (0, 1):
+            ref = fg_piece(p, rel, -1 if dr == 0 else 1)
+            arrive(ref, xg_s.at[dr, rel, p], xg_r.at[dr, rel, p], x_to[1 - dr])
+            if p % 2 == dr:
+                send(ref, ref, xh_s.at[rel, p], xh_r.at[rel, p], x_to[dr])
+
+    for p in (0, 1, 2):
+        fg_own(p)
     for h in (0, 1):
         mine = p2_sum(0, h)
         arrive(yr.at[h], yb_s.at[h], yb_r.at[h], y_to)
@@ -425,31 +473,15 @@
     for i in range(1, 8):
         send(bs.at[flip(FLIPS[i])], br.at[e], cb_s.at[i], cb_r.at[i], c_to[i])
     br[e] = bs[e]
-    zg_all(3, 0)
-
-    def final(t, c):
-        a, b = c * half, (c + 1) * half
-        for dr in (0, 1):
-            zg_arrive(dr, 3, t, c)
-        total = grad[t, s, :, a:b]
-        for dr in (0, 1):
-            total = total + zr[dr, 3, t, :, a:b].astype(F32)
-        fg[t][dp, :, a:b] = total.astype(BF)
-
-    def late(t, rel, k):
-        return fg[t].at[dpx(rel, k), :, pl.ds(half, half)]
-
-    def fg_send_x(rel, t):
-        for dr in (0, 1):
-            ref = late(t, rel, 0)
-            send(ref, ref, xg_s.at[dr, rel, t], xg_r.at[dr, rel, t], x_to[dr])
-
-    for t in range(3):
-        final(t, 1)
-        ref = late(t, 0, 0)
-        send(ref, ref, yg_s.at[t], yg_r.at[t], y_to)
-        fg_send_x(0, t)
-
+    for p in (0, 1, 2):
+        fg_y(p)
+    for p in (3, 4, 5):
+        fg_own(p)
+    for rel in (0, 1):
+        for p in (0, 1, 2):
+            fg_x(p, rel)
+    for p in (3, 4):
+        fg_y(p)
     for i in range(1, 8):
         arrive(br.at[flip(FLIPS[i])], cb_s.at[i], cb_r.at[i], c_to[i])
     gi_ref[...] = lax.dot_general(
@@ -458,57 +490,25 @@
         (((0,), (0,)), ((), ())),
         preferred_element_type=F32,
     ).astype(BF)
-
-    for t in range(3):
-        arrive(late(t, 1, 0), yg_s.at[t], yg_r.at[t], y_to)
-        fg_send_x(1, t)
-    for t in range(3):
-        final(t, 0)
-        ref = fg[t].at[dp, :, pl.ds(0, half)]
-        for i, to in enumerate(all_to):
-            send(ref, ref, dg_s.at[t, i], dg_r.at[t, i], to)
-
-    def relayed(t, rel, k, dr):
-        if t < 2:
-            return late(t, rel, k), t
-        return fg[t].at[dpx(rel, k), :, pl.ds(half + dr * (half // 2), half // 2)], 2 + dr
-
     for rel in (0, 1):
-        for t in range(3):
-            for dr in (0, 1):
-                k = -1 if dr == 0 else 1
-                arrive(late(t, rel, k), xg_s.at[dr, rel, t], xg_r.at[dr, rel, t], x_to[1 - dr])
-                if t == 2 or t == dr:
-                    ref, i = relayed(t, rel, k, dr)
-                    send(ref, ref, xh_s.at[rel, i], xh_r.at[rel, i], x_to[dr])
+        for p in (3, 4):
+            fg_x(p, rel)
     for rel in (0, 1):
-        for t in range(3):
-            for dr in (0, 1):
-                if t == 2 or t == dr:
-                    ref, i = relayed(t, rel, 2, dr)
-                    arrive(ref, xh_s.at[rel, i], xh_r.at[rel, i], x_to[1 - dr])
-    for t in range(3):
-        for i, (rel, k) in enumerate(ALL):
-            arrive(
-                fg[t].at[dpx(rel, -k), :, pl.ds(0, half)], dg_s.at[t, i], dg_r.at[t, i], (dpx(rel, -k), ex)
-            )
+        for p in range(5):
+            arrive(fg_piece(p, rel, 2), xh_s.at[rel, p], xh_r.at[rel, p], x_to[1 - p % 2])
+    for i, (rel, k) in enumerate(ALL):
+        arrive(fg_piece(5, rel, -k), dg_s.at[i], dg_r.at[i], (dpx(rel, -k), ex))
     for c in sends:
         c.wait_send()
 
 
-def finish(gi, gg, gu, gd, gi_out, gg_out, gu_out, gd_out, inner, turned, in_sem, out_sem):
-    refs = [(gg, gg_out), (gu, gu_out), (gi, gi_out), (gd, gd_out)]
-    ins = [pltpu.make_async_copy(a, inner.at[i], in_sem.at[i]) for i, (a, _) in enumerate(refs)]
-    for c in ins:
+def finish(gi, gg, gu, gd, gi_out, gg_out, gu_out, gd_out, turned, sem):
+    outs = [pltpu.make_async_copy(gi, gi_out, sem.at[0]), pltpu.make_async_copy(gd, gd_out, sem.at[1])]
+    for c in outs:
         c.start()
-    outs = []
-    for i, (_, b) in enumerate(refs):
-        ins[i].wait()
-        src = inner.at[i]
-        if i < 2:
-            turned[i] = inner[i].T
-            src = turned.at[i]
-        c = pltpu.make_async_copy(src, b, out_sem.at[i])
+    for i, (src, dst) in enumerate(((gg, gg_out), (gu, gu_out))):
+        turned[i] = src[...].T
+        c = pltpu.make_async_copy(turned.at[i], dst, sem.at[2 + i])
         c.start()
         outs.append(c)
     for c in outs:
@@ -530,9 +530,11 @@
             grad,
             grad,
         ),
-        in_specs=[v, v, a, a, a, a, a],
+        in_specs=[a] * 7,
         out_specs=(v, v, v, v),
         scratch_shapes=[
+            vm((8, 128), jnp.int32),
+            vm((8, 128), F32),
             vm((rows, width), BF),
             vm((rows, width), BF),
             vm((width, hid), BF),
@@ -554,7 +556,7 @@
             vm((2, 32, width), BF),
             vm((8, 8, width), BF),
             vm((8, 8, width), BF),
-            DMA((5,)),
+            DMA((7,)),
             DMA((2, 4, 3)),
             DMA((2, 4, 3)),
             DMA((8,)),
@@ -577,34 +579,34 @@
             DMA((2,)),
             DMA((8,)),
             DMA((8,)),
-            DMA((3,)),
-            DMA((3,)),
-            DMA((2, 2, 3)),
-            DMA((2, 2, 3)),
-            DMA((2, 4)),
-            DMA((2, 4)),
-            DMA((3, 7)),
-            DMA((3, 7)),
+            DMA((5,)),
+            DMA((5,)),
+            DMA((2, 2, 5)),
+            DMA((2, 2, 5)),
+            DMA((2, 5)),
+            DMA((2, 5)),
+            DMA((7,)),
+            DMA((7,)),
         ],
         compiler_params=pltpu.CompilerParams(
-            collective_id=0, has_side_effects=True, vmem_limit_bytes=60 * 1024 * 1024
+            collective_id=0, has_side_effects=True, vmem_limit_bytes=40 * 1024 * 1024
         ),
-    )(expert_ids.T, gate_probs.T, tokens, cotangent, gate_weight, up_weight, down_weight)
+    )(
+        *[
+            pltpu.with_memory_space_constraint(i, pltpu.MemorySpace.HBM)
+            for i in (expert_ids.T, gate_probs.T, tokens, cotangent, gate_weight, up_weight, down_weight)
+        ],
+    )
     flat = jax.ShapeDtypeStruct((hid, width), BF)
     tall = jax.ShapeDtypeStruct((width, hid), BF)
     grads = [g.reshape(hid, width) for g in grads]
     grad_input, gate, up, down = pl.pallas_call(
         finish,
         out_shape=(flat, tall, tall, flat),
-        in_specs=[a] * 4,
+        in_specs=[v] * 4,
         out_specs=(a, a, a, a),
-        scratch_shapes=[
-            vm((4, hid, width), BF),
-            vm((2, width, hid), BF),
-            DMA((4,)),
-            DMA((4,)),
-        ],
-        compiler_params=pltpu.CompilerParams(vmem_limit_bytes=60 * 1024 * 1024),
+        scratch_shapes=[vm((2, width, hid), BF), DMA((4,))],
+        compiler_params=pltpu.CompilerParams(vmem_limit_bytes=40 * 1024 * 1024),
     )(grad_input, *grads)
     return (grad_input, gate[None], up[None], down[None])
 

time: 117 us -> 114 us (0.974)
  the two profiles are of different devices: /device:TPU:1 before, /device:TPU:6 now
where the time goes in v5:
time: 114 us; the launch traced here: 113 us
  Pallas kernels  113 us (99%)
    pallas_call x1, Pallas kernels, local(): pl.pallas_call(kernel, out_shape=(jax.ShapeDtypeStruct((rows, width), BF)...  111 us

profile of v5, /device:TPU:6, one launch (start us, length us, event | category | flops | bytes accessed | tf_op | source)
XLA Modules:
  0.0 113.4 jit_solution(1334580652661123334)
XLA Ops:
  0.6 111.4 %shard_map.102 = (bf16[128,2048]{1,0:T(8,128)(2,1)S(1)}, bf16[8,16,2048]{2,1,0:T(8,128)(2,1)S(1)}, bf16[8,16,2048]{2,1,0:T(8,128)(2,1)S(1)}, bf16[8,16,2048]{2,1,0:T(8,128)(2,1)S(1)}) custom-call(s32[8,128]{1,0:T(8,128)} %bitcast.11, f32[8,128]{1,0:T(8,128)} %bitcast.12, bf16[128,2048]{1,0:T(8,128)(2,1)} %tok_hbm.1, bf16[128,2048]{1,0:T(8,128)(2,1)} %cot_hbm.1, ...), custom_call_target="tpu_custom_call" | custom-call | tf_op jit(solution)/shard_map/pallas_call | solution.py:525
  112.0 1.3 %shard_map.103 = (bf16[128,2048]{1,0:T(8,128)(2,1)}, bf16[2048,128]{1,0:T(8,128)(2,1)}, bf16[2048,128]{1,0:T(8,128)(2,1)}, bf16[128,2048]{1,0:T(8,128)(2,1)}) custom-call(bf16[128,2048]{1,0:T(8,128)(2,1)S(1)} %get-tuple-element.12.gi, bf16[128,2048]{1,0:T(8,128)(2,1)S(1)} %bitcast.8, bf16[128,2048]{1,0:T(8,128)(2,1)S(1)} %bitcast.9, ...), custom_call_target="tpu_custom_call" | custom-call | tf_op jit(solution)/shard_map/pallas_call | solution.py:603

commit v6 on v5

--- a/solution.py
+++ b/solution.py
@@ -82,6 +82,8 @@
     xh_r,
     dg_s,
     dg_r,
+    yq_s,
+    yq_r,
 ):
     fg = (gg_ref, gu_ref, gd_ref)
     width = tok.shape[1]
@@ -307,7 +309,7 @@
         zero = jnp.zeros_like(active)
         top = jnp.concatenate([dgate, dupward, zero], axis=2)
         low = jnp.concatenate([zero, zero, active], axis=2)
-        both = jnp.concatenate([top[:, None], low[:, None]], axis=1).reshape(256, 384).T.astype(BF)
+        both = jnp.concatenate([top[:, None], low[:, None]], axis=1).reshape(256, 384).astype(BF).T
         pairs = top.reshape(128, 384)[:, :256].astype(BF)
         for i in (0, 1):
             lt[:, pl.ds(pl.multiple_of(d[i] * 128, 128), 128)] = both[:, i * 128 : (i + 1) * 128]
@@ -329,7 +331,7 @@
     yx_in(2, 2)
     compute(2)
 
-    tile = 256
+    tile = 512
 
     def grad_tile(n, carry):
         cols = pl.ds(pl.multiple_of(n * tile, tile), tile)
@@ -356,7 +358,7 @@
 
     steps = width // tile // 2
     for c in (0, 1):
-        lax.fori_loop(c * steps, (c + 1) * steps, grad_tile, 0)
+        lax.fori_loop(c * steps, (c + 1) * steps, grad_tile, 0, unroll=True)
         for t in range(3):
             zg(c, 0, t, c, False)
         for t in range(3):
@@ -371,7 +373,7 @@
         part[pl.ds(i * 2, 2)] = p.reshape(2, 64, width)
         return carry
 
-    lax.fori_loop(0, 4, part_tile, 0)
+    lax.fori_loop(0, 4, part_tile, 0, unroll=True)
 
     for rel in (1, 0):
         for dr in (0, 1):
@@ -454,7 +456,17 @@
 
     def fg_y(p):
         arrive(fg_piece(p, 1, 0), yg_s.at[p], yg_r.at[p], y_to)
-        fg_send_x(p, 1)
+        if p >= 2:
+            fg_send_x(p, 1)
+
+    def fg_down(p, i, k):
+        ref = fg_piece(p, 0, k)
+        send(ref, ref, yq_s.at[p, i], yq_r.at[p, i], y_to)
+
+    def fg_far(p, rel):
+        arrive(fg_piece(p, rel, 2), xh_s.at[rel, p], xh_r.at[rel, p], x_to[1 - p % 2])
+        if p < 2:
+            fg_down(p, 2, 2)
 
     def fg_x(p, rel):
         for dr in (0, 1):
@@ -462,6 +474,8 @@
             arrive(ref, xg_s.at[dr, rel, p], xg_r.at[dr, rel, p], x_to[1 - dr])
             if p % 2 == dr:
                 send(ref, ref, xh_s.at[rel, p], xh_r.at[rel, p], x_to[dr])
+            if p < 2:
+                fg_down(p, dr, -1 if dr == 0 else 1)
 
     for p in (0, 1, 2):
         fg_own(p)
@@ -473,13 +487,16 @@
     for i in range(1, 8):
         send(bs.at[flip(FLIPS[i])], br.at[e], cb_s.at[i], cb_r.at[i], c_to[i])
     br[e] = bs[e]
-    for p in (0, 1, 2):
-        fg_y(p)
-    for p in (3, 4, 5):
-        fg_own(p)
-    for rel in (0, 1):
-        for p in (0, 1, 2):
-            fg_x(p, rel)
+    fg_x(0, 0)
+    fg_x(1, 0)
+    fg_y(2)
+    fg_own(3)
+    fg_far(0, 0)
+    fg_far(1, 0)
+    fg_own(4)
+    fg_own(5)
+    fg_x(2, 0)
+    fg_x(2, 1)
     for p in (3, 4):
         fg_y(p)
     for i in range(1, 8):
@@ -494,8 +511,12 @@
         for p in (3, 4):
             fg_x(p, rel)
     for rel in (0, 1):
-        for p in range(5):
-            arrive(fg_piece(p, rel, 2), xh_s.at[rel, p], xh_r.at[rel, p], x_to[1 - p % 2])
+        for p in (2, 3, 4):
+            fg_far(p, rel)
+    for p in (0, 1):
+        fg_y(p)
+        for i, k in enumerate((-1, 1, 2)):
+            arrive(fg_piece(p, 1, k), yq_s.at[p, i], yq_r.at[p, i], y_to)
     for i, (rel, k) in enumerate(ALL):
         arrive(fg_piece(5, rel, -k), dg_s.at[i], dg_r.at[i], (dpx(rel, -k), ex))
     for c in sends:
@@ -587,6 +608,8 @@
             DMA((2, 5)),
             DMA((7,)),
             DMA((7,)),
+            DMA((2, 3)),
+            DMA((2, 3)),
         ],
         compiler_params=pltpu.CompilerParams(
             collective_id=0, has_side_effects=True, vmem_limit_bytes=40 * 1024 * 1024

time: 114 us -> 113 us (level)
  no operation moved by 1% of the time
where the time goes in v6:
time: 113 us
  Pallas kernels  113 us (100%)
    pallas_call x1, Pallas kernels, local(): pl.pallas_call(kernel, out_shape=(jax.ShapeDtypeStruct((rows, width), BF)...  111 us

profile of v6, /device:TPU:6, one launch (start us, length us, event | category | flops | bytes accessed | tf_op | source)
XLA Modules:
  0.0 113.2 jit_solution(18275588693153365171)
XLA Ops:
  0.6 111.2 %shard_map.102 = (bf16[128,2048]{1,0:T(8,128)(2,1)S(1)}, bf16[8,16,2048]{2,1,0:T(8,128)(2,1)S(1)}, bf16[8,16,2048]{2,1,0:T(8,128)(2,1)S(1)}, bf16[8,16,2048]{2,1,0:T(8,128)(2,1)S(1)}) custom-call(s32[8,128]{1,0:T(8,128)} %bitcast.11, f32[8,128]{1,0:T(8,128)} %bitcast.12, bf16[128,2048]{1,0:T(8,128)(2,1)} %tok_hbm.1, bf16[128,2048]{1,0:T(8,128)(2,1)} %cot_hbm.1, ...), custom_call_target="tpu_custom_call" | custom-call | tf_op jit(solution)/shard_map/pallas_call | solution.py:546
  111.8 1.3 %shard_map.103 = (bf16[128,2048]{1,0:T(8,128)(2,1)}, bf16[2048,128]{1,0:T(8,128)(2,1)}, bf16[2048,128]{1,0:T(8,128)(2,1)}, bf16[128,2048]{1,0:T(8,128)(2,1)}) custom-call(bf16[128,2048]{1,0:T(8,128)(2,1)S(1)} %get-tuple-element.12.gi, bf16[128,2048]{1,0:T(8,128)(2,1)S(1)} %bitcast.8, bf16[128,2048]{1,0:T(8,128)(2,1)S(1)} %bitcast.9, ...), custom_call_target="tpu_custom_call" | custom-call | tf_op jit(solution)/shard_map/pallas_call | solution.py:626
